TPU v7x, 256 devices: a whole 4x4x8 slice. The times are simulated.
256 devices in a mesh: cell: 64 (over x, z, y_hi), gene: 4 (over y_lo, core).
Axes of the slice: x: 4, y: 4 (y_hi: 2, y_lo: 2; y = y_hi * 2 + y_lo), z: 8, core: 2. Of those that a mesh axis runs over, the one named last changes fastest.
Arguments:
- counts: int32 [16384, 4096], P('cell', 'gene'), may hold values from 0 to 7
- totals: int32 [16384], P('cell'), may hold values from 1000 to 19999
- cell_factors: float32 [16384, 32], P('cell'), may hold values from -0.9 to 0.9
- gene_loadings: float32 [4096, 32], P('gene'), may hold values from -0.9 to 0.9
Outputs:
- new_factors: float32 [16384, 32], P('cell')
- new_loadings: float32 [4096, 32], P('gene')
- deviance: float32 [4096], P('gene')
All inputs are finite; a program needn't handle non-finite values.
Results may differ from a plain program's by a relative error of at most 0.0044.
Values sent between devices are 32-bit elements; how exact they have to be, the bound alone decides.
A program may use at most 128 MiB of HBM per device.

v0:
```python
import math

import jax
import jax.numpy as jnp
from jax import lax
from jax.sharding import PartitionSpec as P

RIDGE = 1.0
DAMPING = 0.1
SCALE_TOTAL = 5000.0


def joined_along(pieces, dim):
    pieces = jnp.moveaxis(pieces, 0, dim)
    dims = pieces.shape
    return pieces.reshape(*dims[:dim], dims[dim] * dims[dim + 1], *dims[dim + 2 :])


def copy_for_each(shard, axis):
    size = lax.axis_size(axis)
    return lax.all_to_all(
        jnp.broadcast_to(shard[None], (size, *shard.shape)), axis, 0, 0, tiled=True
    )


def gather_directly(shard, axis, dim):
    return joined_along(copy_for_each(shard, axis), dim)


def outer_table(factors):
    width = factors.shape[1]
    product = factors[:, :, None] * factors[:, None, :]
    return product.reshape(factors.shape[0], width * width).astype(jnp.bfloat16)


def newton_solve(curvature, gradient):
    width = gradient.shape[1]
    matrix = jnp.transpose(curvature.reshape(gradient.shape[0], width, width), (1, 2, 0))
    diagonal_mean = sum((matrix[index, index] for index in range(width))) / width
    shift = RIDGE + DAMPING * diagonal_mean
    right = jnp.transpose(gradient)
    columns = []
    for column in range(width):
        current = matrix[:, column]
        if column > 0:
            stacked = jnp.stack(columns)
            current = current - jnp.sum(stacked * stacked[:, column][:, None, :], axis=0)
        current = (
            current
            + jnp.where(jnp.arange(width) == column, 1.0, 0.0).astype(jnp.float32)[:, None]
            * shift[None, :]
        )
        pivot = jnp.sqrt(current[column])
        mask = (jnp.arange(width) >= column).astype(jnp.float32)[:, None]
        columns.append(mask * current / pivot[None, :])
    lower = jnp.stack(columns, axis=1)
    forward = []
    for row in range(width):
        value = right[row]
        for inner in range(row):
            value = value - lower[row, inner] * forward[inner]
        forward.append(value / lower[row, row])
    backward = [None] * width
    for row in range(width - 1, -1, -1):
        value = forward[row]
        for inner in range(row + 1, width):
            value = value - lower[inner, row] * backward[inner]
        backward[row] = value / lower[row, row]
    return jnp.transpose(jnp.stack(backward))


def predict(offset, factors, loadings):
    linear = offset[:, None] + jnp.dot(factors, loadings.T, precision=lax.Precision.HIGHEST)
    return (linear, jnp.exp(linear))


def gene_contract(counts, expected, loadings, table_maker):
    weights = expected.astype(jnp.bfloat16)
    residual = (counts.astype(jnp.float32) - expected).astype(jnp.bfloat16)
    gradient = jnp.dot(residual, loadings.astype(jnp.bfloat16), preferred_element_type=jnp.float32)
    curvature = jnp.dot(weights, table_maker(loadings), preferred_element_type=jnp.float32)
    return (gradient, curvature)


def cell_contract(counts, linear, expected, factors, table_maker):
    counts_real = counts.astype(jnp.float32)
    weights = expected.astype(jnp.bfloat16)
    residual = (counts_real - expected).astype(jnp.bfloat16)
    dims = (((0,), (0,)), ((), ()))
    gradient = lax.dot_general(
        residual, factors.astype(jnp.bfloat16), dims, preferred_element_type=jnp.float32
    )
    curvature = lax.dot_general(
        weights, table_maker(factors), dims, preferred_element_type=jnp.float32
    )
    terms = 2.0 * (
        counts_real * (jnp.log(jnp.maximum(counts_real, 1.0)) - linear) - counts_real + expected
    )
    return (gradient, curvature, jnp.sum(terms, axis=0))


def on_device(counts, totals, cell_factors, gene_loadings):
    offset = jnp.log(totals.astype(jnp.float32)) - math.log(SCALE_TOTAL)
    regrouped = lax.all_to_all(counts, "gene", split_axis=0, concat_axis=1, tiled=True)
    portion = regrouped.shape[0]
    start_row = lax.axis_index("gene") * portion
    row_offset = lax.dynamic_slice_in_dim(offset, start_row, portion, 0)
    row_factors = lax.dynamic_slice_in_dim(cell_factors, start_row, portion, 0)
    loading_piece = gather_directly(gene_loadings, "gene", 0)
    linear_piece, expected_piece = predict(row_offset, row_factors, loading_piece)
    gradient_piece, curvature_piece = gene_contract(
        regrouped, expected_piece, loading_piece, outer_table
    )
    gradient_sum = gradient_piece
    curvature_sum = curvature_piece
    row_new = row_factors + newton_solve(curvature_sum, gradient_sum - RIDGE * row_factors)
    new_factors = gather_directly(row_new, "gene", 0)
    cell_total = counts.shape[0] * lax.axis_size("cell")
    linear_next, expected_next = predict(offset, new_factors, gene_loadings)
    gradient_part, curvature_part, deviance_part = cell_contract(
        counts, linear_next, expected_next, new_factors, outer_table
    )
    gradient_sum, curvature_sum, deviance_sum = lax.psum(
        (gradient_part, curvature_part, deviance_part), "cell"
    )
    new_loadings = gene_loadings + newton_solve(curvature_sum, gradient_sum - RIDGE * gene_loadings)
    deviance = deviance_sum / cell_total
    return (new_factors, new_loadings, deviance)


def solution(mesh):
    return jax.shard_map(
        on_device,
        mesh=mesh,
        in_specs=(P("cell", "gene"), P("cell"), P("cell", None), P("gene", None)),
        out_specs=(P("cell", None), P("gene", None), P("gene")),
        check_vma=False,
    )
```

profile of v0, /device:TPU:8, one launch (start us, length us, event | category | flops | bytes accessed | tf_op | source)
XLA Modules:
  0.0 906.9 jit_solution(10834958281265246172)
XLA Ops:
  7.2 1.8 broadcast_in_dim.138
  8.9 5.6 all-to-all-start.1
  22.8 4.1 all-to-all-start
  26.9 1.1 fusion.5
  28.1 2.3 fusion.1
  56.3 5.4 all_to_all.23
  63.1 2.1 fusion.9
  67.1 4.5 copy.291
  71.6 184.9 %psum.23 = f32[1024]{0:T(1024)S(1)} all-reduce(f32[1024]{0:T(1024)S(1)} %get-tuple-element.1857), channel_id=1, replica_groups=mesh['cell'=64,'gene'=4] {'cell'}, use_global_device_ids=true, to_apply=%region_63.64 | all-reduce | flops 1024 | bytes 8192 | tf_op jit(solution)/shard_map/psum | solution.py:123
  257.2 519.9 %all-reduce.3.cloned.1.call-done = (f32[32,32,1024]{2,0,1:T(8,128)}, f32[1024,32]{0,1:T(8,128)}) async-done(((f32[32,32,1024]{2,0,1:T(8,128)}, f32[1024,32]{0,1:T(8,128)}), (f32[32,32,1024]{2,0,1:T(8,128)}, f32[1024,32]{0,1:T(8,128)})) %all-reduce.3.cloned.1.call-update) | async-done | bytes 4325392 | tf_op jit(solution)/shard_map/psum | solution.py:123
  780.4 1.1 constant_dynamic-update-slice_fusion.940
  781.5 1.7 fusion.139
  784.0 2.4 constant_dynamic-update-slice_fusion.971
  787.3 1.4 multiply_divide_fusion.28
  789.7 1.2 fusion.133
  790.9 1.4 multiply_divide_fusion.27
  803.3 1.3 multiply_reduce_fusion.23
  819.3 1.6 multiply_reduce_fusion.19
  839.9 1.7 multiply_reduce_fusion.18
  843.0 1.2 copy-done.3
  844.4 1.7 multiply_reduce_fusion.17
  848.6 1.8 multiply_reduce_fusion.16
  855.0 1.9 multiply_reduce_fusion.14
  859.3 1.9 multiply_reduce_fusion.13
  862.4 1.3 slice.8616
  863.7 2.0 multiply_reduce_fusion.12
  878.1 7.1 subtract_divide_fusion.12
  887.8 2.1 subtract_divide_fusion
  891.3 1.8 subtract_divide_fusion.81
  893.3 1.7 subtract_divide_fusion.74
  895.0 1.3 subtract_divide_fusion.57
  896.3 2.2 subtract_divide_fusion.48
  (956 shorter events, 114.0 us)
Async XLA Ops:
  8.9 13.8 %all-to-all-start.1 = ((f32[4,1024,32]{1,2,0:T(8,128)}), f32[4,1024,32]{1,2,0:T(8,128)S(1)}, u32[]{:S(2)}, u32[]{:S(2)}) async-start(f32[4,1024,32]{1,2,0:T(8,128)} %broadcast_in_dim.138), calls=%async_computation.1 | async-start | bytes 1048576 | tf_op jit(solution)/shard_map/all_to_all | solution.py:21
  20.2 25.2 %copy-start.131 = (f32[32]{0:T(128)}, f32[32]{0:T(128)S(1)}, u32[]{:S(2)}) copy-start(f32[32]{0:T(128)S(1)} %compare_select_fusion.14) | copy-start | bytes 388
  20.3 25.5 %copy-start.127 = (f32[32]{0:T(128)}, f32[32]{0:T(128)S(1)}, u32[]{:S(2)}) copy-start(f32[32]{0:T(128)S(1)} %compare_select_fusion.13) | copy-start | bytes 388
  20.3 25.4 %copy-start.129 = (f32[32]{0:T(128)}, f32[32]{0:T(128)S(1)}, u32[]{:S(2)}) copy-start(f32[32]{0:T(128)S(1)} %compare_convert_fusion.13) | copy-start | bytes 388
  20.3 25.8 %copy-start.123 = (f32[32]{0:T(128)}, f32[32]{0:T(128)S(1)}, u32[]{:S(2)}) copy-start(f32[32]{0:T(128)S(1)} %compare_select_fusion.12) | copy-start | bytes 388
  20.3 25.8 %copy-start.125 = (f32[32]{0:T(128)}, f32[32]{0:T(128)S(1)}, u32[]{:S(2)}) copy-start(f32[32]{0:T(128)S(1)} %compare_convert_fusion.12) | copy-start | bytes 388
  20.4 26.1 %copy-start.119 = (f32[32]{0:T(128)}, f32[32]{0:T(128)S(1)}, u32[]{:S(2)}) copy-start(f32[32]{0:T(128)S(1)} %compare_select_fusion.11) | copy-start | bytes 388
  20.4 26.1 %copy-start.121 = (f32[32]{0:T(128)}, f32[32]{0:T(128)S(1)}, u32[]{:S(2)}) copy-start(f32[32]{0:T(128)S(1)} %compare_convert_fusion.11) | copy-start | bytes 388
  20.4 26.4 %copy-start.115 = (f32[32]{0:T(128)}, f32[32]{0:T(128)S(1)}, u32[]{:S(2)}) copy-start(f32[32]{0:T(128)S(1)} %compare_select_fusion.10) | copy-start | bytes 388
  20.4 26.4 %copy-start.117 = (f32[32]{0:T(128)}, f32[32]{0:T(128)S(1)}, u32[]{:S(2)}) copy-start(f32[32]{0:T(128)S(1)} %compare_convert_fusion.10) | copy-start | bytes 388
  20.4 26.7 %copy-start.111 = (f32[32]{0:T(128)}, f32[32]{0:T(128)S(1)}, u32[]{:S(2)}) copy-start(f32[32]{0:T(128)S(1)} %compare_select_fusion.9) | copy-start | bytes 388
  20.5 26.7 %copy-start.113 = (f32[32]{0:T(128)}, f32[32]{0:T(128)S(1)}, u32[]{:S(2)}) copy-start(f32[32]{0:T(128)S(1)} %compare_convert_fusion.9) | copy-start | bytes 388
  20.5 27.0 %copy-start.107 = (f32[32]{0:T(128)}, f32[32]{0:T(128)S(1)}, u32[]{:S(2)}) copy-start(f32[32]{0:T(128)S(1)} %compare_select_fusion.8) | copy-start | bytes 388
  20.5 27.0 %copy-start.109 = (f32[32]{0:T(128)}, f32[32]{0:T(128)S(1)}, u32[]{:S(2)}) copy-start(f32[32]{0:T(128)S(1)} %compare_convert_fusion.8) | copy-start | bytes 388
  20.5 27.3 %copy-start.103 = (f32[32]{0:T(128)}, f32[32]{0:T(128)S(1)}, u32[]{:S(2)}) copy-start(f32[32]{0:T(128)S(1)} %compare_select_fusion.7) | copy-start | bytes 388
  20.5 27.3 %copy-start.105 = (f32[32]{0:T(128)}, f32[32]{0:T(128)S(1)}, u32[]{:S(2)}) copy-start(f32[32]{0:T(128)S(1)} %compare_convert_fusion.7) | copy-start | bytes 388
  20.6 27.7 %copy-start.99 = (f32[32]{0:T(128)}, f32[32]{0:T(128)S(1)}, u32[]{:S(2)}) copy-start(f32[32]{0:T(128)S(1)} %compare_select_fusion.6) | copy-start | bytes 388
  20.6 27.6 %copy-start.101 = (f32[32]{0:T(128)}, f32[32]{0:T(128)S(1)}, u32[]{:S(2)}) copy-start(f32[32]{0:T(128)S(1)} %compare_convert_fusion.6) | copy-start | bytes 388
  20.6 28.0 %copy-start.95 = (f32[32]{0:T(128)}, f32[32]{0:T(128)S(1)}, u32[]{:S(2)}) copy-start(f32[32]{0:T(128)S(1)} %compare_select_fusion.5) | copy-start | bytes 388
  20.6 28.0 %copy-start.97 = (f32[32]{0:T(128)}, f32[32]{0:T(128)S(1)}, u32[]{:S(2)}) copy-start(f32[32]{0:T(128)S(1)} %compare_convert_fusion.5) | copy-start | bytes 388
  20.6 28.3 %copy-start.91 = (f32[32]{0:T(128)}, f32[32]{0:T(128)S(1)}, u32[]{:S(2)}) copy-start(f32[32]{0:T(128)S(1)} %compare_select_fusion.4) | copy-start | bytes 388
  20.7 28.3 %copy-start.93 = (f32[32]{0:T(128)}, f32[32]{0:T(128)S(1)}, u32[]{:S(2)}) copy-start(f32[32]{0:T(128)S(1)} %compare_convert_fusion.4) | copy-start | bytes 388
  20.7 28.6 %copy-start.87 = (f32[32]{0:T(128)}, f32[32]{0:T(128)S(1)}, u32[]{:S(2)}) copy-start(f32[32]{0:T(128)S(1)} %compare_select_fusion.3) | copy-start | bytes 388
  20.7 28.6 %copy-start.89 = (f32[32]{0:T(128)}, f32[32]{0:T(128)S(1)}, u32[]{:S(2)}) copy-start(f32[32]{0:T(128)S(1)} %compare_convert_fusion.3) | copy-start | bytes 388
  20.7 29.0 %copy-start.83 = (f32[32]{0:T(128)}, f32[32]{0:T(128)S(1)}, u32[]{:S(2)}) copy-start(f32[32]{0:T(128)S(1)} %compare_select_fusion.2) | copy-start | bytes 388
  22.2 27.5 %copy-start.85 = (f32[32]{0:T(128)}, f32[32]{0:T(128)S(1)}, u32[]{:S(2)}) copy-start(f32[32]{0:T(128)S(1)} %compare_convert_fusion.2) | copy-start | bytes 388
  22.2 27.9 %copy-start.79 = (f32[32]{0:T(128)}, f32[32]{0:T(128)S(1)}, u32[]{:S(2)}) copy-start(f32[32]{0:T(128)S(1)} %compare_select_fusion.1) | copy-start | bytes 388
  22.2 27.9 %copy-start.81 = (f32[32]{0:T(128)}, f32[32]{0:T(128)S(1)}, u32[]{:S(2)}) copy-start(f32[32]{0:T(128)S(1)} %compare_convert_fusion.1) | copy-start | bytes 388
  22.8 29.7 %all-to-all-start = ((s32[4,64,1024]{2,1,0:T(8,128)}), s32[4,64,1024]{2,1,0:T(8,128)S(1)}, u32[]{:S(2)}, u32[]{:S(2)}) async-start(s32[4,64,1024]{2,1,0:T(8,128)} %bitcast.8741), calls=%async_computation | async-start | bytes 2097152 | tf_op jit(solution)/shard_map/all_to_all | solution.py:104
  26.9 750.2 %all-reduce.3.cloned.1.call-start = ((), (), s32[]{:S(2)}) async-start(), calls=%async_computation.3 | async-start | bytes 8650752 | tf_op jit(solution)/shard_map/psum | solution.py:123
  841.9 35.6 %copy-start.33 = (f32[32,1024]{1,0:T(8,128)}, f32[32,1024]{1,0:T(8,128)S(1)}, u32[]{:S(2)}) copy-start(f32[32,1024]{1,0:T(8,128)S(1)} %multiply_divide_fusion.17) | copy-start | bytes 393220
  846.3 31.3 %copy-start.34 = (f32[32,1024]{1,0:T(8,128)}, f32[32,1024]{1,0:T(8,128)S(1)}, u32[]{:S(2)}) copy-start(f32[32,1024]{1,0:T(8,128)S(1)} %multiply_divide_fusion.16) | copy-start | bytes 393220
  (129 other events, 804.5 us)
Sparse Core Ops, SparseCore 0:
  71.8 705.2 all-reduce.2
where the time goes:
time: 923 us; the launch traced here: 907 us
  waiting for transfers between devices  520 us (56%)
  blocking collectives  190 us (21%)
  other arithmetic  99.4 us (11%)
  local copies, waits for them, and re-layouts  60.9 us (7%)
  between operations  19.1 us (2%)
  starting transfers between devices  9.67 us (1%)
    psum x1, waiting for transfers between devices, on_device(): lax.psum((gradient_part, curvature_part, deviance_part), 'cell')  520 us
    psum x1, blocking collectives, on_device(): lax.psum((gradient_part, curvature_part, deviance_part), 'cell')  185 us
    unnamed x448, local copies, waits for them, and re-layouts  30.5 us
    reduce_sum x60, other arithmetic, newton_solve(): jnp.sum(stacked * stacked[:, column][:, None, :], axis=0)  21.6 us
  transfers between devices with their start and end apart: 3, of which 1 were waited for; matrix products, arithmetic and copies ran while one was open for 4% of the time, Pallas kernels for 0%

commit v1 on v0

v1 whole, which is shorter than its diff:
```python
import math

import jax
import jax.numpy as jnp
from jax import lax
from jax.experimental import pallas as pl
from jax.experimental.pallas import tpu as pltpu
from jax.sharding import PartitionSpec as P

F32, BF16 = jnp.float32, jnp.bfloat16
MESH = pl.DeviceIdType.MESH

RIDGE = 1.0
DAMPING = 0.1
LOG_SCALE = math.log(5000.0)

WIDTH = 32
X, Z, YH = 4, 8, 2
CELL_DEVICES = X * Z * YH
T = X * YH
CELLS = 256
GENES = 1024
LANES = 128
GENES_Z = GENES // Z
OWN_GENES = GENES_Z // T
HALF = LANES // 2

HEIGHT = [WIDTH - c // 8 * 8 for c in range(WIDTH)]
START = [sum(HEIGHT[:c]) for c in range(WIDTH)]
TRIANGLE = sum(HEIGHT)
ROWS1 = TRIANGLE + WIDTH
ROWS2 = 704
PIECE2 = ROWS2 // T


def parts_of(value):
    high = value.astype(BF16).astype(F32)
    rest = value - high
    middle = rest.astype(BF16).astype(F32)
    return high, middle, rest - middle


def left_stack(factors, offset):
    high, middle, low = parts_of(factors)
    row = lax.broadcasted_iota(jnp.int32, (16, factors.shape[1]), 0)
    off_high, off_middle, off_low = parts_of(offset)
    extra = jnp.where(
        row == 0, off_high, jnp.where(row == 1, off_middle, jnp.where(row == 2, off_low, 0.0))
    )
    return jnp.concatenate([high, high, middle, middle, high, low, extra], axis=0).astype(BF16)


def right_stack(loadings):
    high, middle, low = parts_of(loadings)
    extra = jnp.ones((16, loadings.shape[1]), F32)
    return jnp.concatenate([high, middle, high, middle, low, high, extra], axis=0).astype(BF16)


def predict(left, right):
    return lax.dot_general(left, right, (((0,), (0,)), ((), ())), preferred_element_type=F32)


def write_table(table_ref, columns, rows):
    for c in range(0, WIDTH, 2):
        first = c // 8 * 8
        pair = jnp.concatenate(
            [rows[first:] * rows[c : c + 1], rows[first:] * rows[c + 1 : c + 2]], axis=0
        )
        table_ref[START[c] : START[c] + 2 * HEIGHT[c], columns] = pair.astype(BF16)
    table_ref[TRIANGLE : TRIANGLE + WIDTH, columns] = rows.astype(BF16)


def solve(matrix_ref, right_ref, column_ref, inverse_ref):
    for j in range(8, WIDTH):
        for block in range(j // 8):
            matrix_ref[WIDTH * j + 8 * block : WIDTH * j + 8 * block + 8, :] = matrix_ref[
                pl.ds(WIDTH * 8 * block + j, 8, stride=WIDTH), :
            ]
    diagonal = matrix_ref[pl.ds(0, WIDTH, stride=WIDTH + 1), :]
    shift = RIDGE + DAMPING * (jnp.sum(diagonal, axis=0, keepdims=True) / WIDTH)
    matrix_ref[pl.ds(0, WIDTH, stride=WIDTH + 1), :] = diagonal + shift
    row = lax.broadcasted_iota(jnp.int32, (WIDTH, LANES), 0)
    for group in range(WIDTH // 8):

        def step(c, carry):
            column = matrix_ref[pl.ds(pl.multiple_of(c * WIDTH, WIDTH), WIDTH), :]
            column_ref[...] = column
            inverse = 1.0 / column_ref[pl.ds(c, 1), :]
            inverse_ref[pl.ds(c, 1), :] = inverse
            scaled = jnp.where(row == c, 0.0, column * inverse)
            right_ref[...] = right_ref[...] - scaled * right_ref[pl.ds(c, 1), :]
            for j in range(8 * group, WIDTH):
                at = slice(WIDTH * j, WIDTH * j + WIDTH)
                matrix_ref[at, :] = matrix_ref[at, :] - scaled * column_ref[j : j + 1, :]
            return carry

        lax.fori_loop(8 * group, 8 * group + 8, step, 0)
    return right_ref[...] * inverse_ref[...]


def load_matrix(matrix_ref, packed_ref):
    for c in range(WIDTH):
        first = WIDTH - HEIGHT[c]
        matrix_ref[WIDTH * c + first : WIDTH * c + WIDTH, :] = packed_ref[
            START[c] : START[c] + HEIGHT[c], :
        ]


def kernel(
    counts_ref, totals_ref, factors_ref, loadings_ref,
    new_factors_ref, new_loadings_ref, deviance_ref,
    loadings_t, factors_t, table1, weights1, residual1, sums1, core_in, yl_out, yl_in,
    packed, matrix, right, column, inverse,
    counts_z, totals_z, factor_slots, table2, both2, sums2, piece_out, piece_in, final_out,
    final_in, final_t,
    counts_send, counts_recv, totals_send, totals_recv, pair_send, pair_recv,
    factor_send, factor_recv, piece_send, piece_recv, final_send, final_recv,
):
    cell = lax.axis_index("cell")
    gene = lax.axis_index("gene")
    x, z, yh = cell // (Z * YH), (cell // YH) % Z, cell % YH
    yl, core = gene // 2, gene % 2
    t = x * YH + yh
    quarter = core * 2 + yl

    def cell_at(x_, z_, yh_):
        return (x_ * Z + z_) * YH + yh_

    barrier = pltpu.get_barrier_semaphore()

    def greet_cell(d, carry):
        pl.semaphore_signal(
            barrier, inc=1, device_id={"cell": (cell + d) % CELL_DEVICES, "gene": gene},
            device_id_type=MESH,
        )
        return carry

    def greet_gene(k, carry):
        pl.semaphore_signal(
            barrier, inc=1,
            device_id={"cell": cell_at(x, k // 3, yh), "gene": (gene + 1 + k % 3) % 4},
            device_id_type=MESH,
        )
        return carry

    lax.fori_loop(1, CELL_DEVICES, greet_cell, 0)
    lax.fori_loop(0, 3 * Z, greet_gene, 0)
    pl.semaphore_wait(barrier, CELL_DEVICES - 1 + 3 * Z)

    def counts_copy(d):
        other = (z + d) % Z
        return pltpu.make_async_remote_copy(
            src_ref=counts_ref.at[:, pl.ds(pl.multiple_of(other * GENES_Z, GENES_Z), GENES_Z)],
            dst_ref=counts_z.at[z],
            send_sem=counts_send.at[d], recv_sem=counts_recv.at[z],
            device_id={"cell": cell_at(x, other, yh), "gene": gene}, device_id_type=MESH,
        )

    def totals_copy(d):
        other = (z + d) % Z
        return pltpu.make_async_remote_copy(
            src_ref=totals_ref, dst_ref=totals_z.at[z],
            send_sem=totals_send.at[d], recv_sem=totals_recv.at[z],
            device_id={"cell": cell_at(x, other, yh), "gene": gene}, device_id_type=MESH,
        )

    def counts_arrived(d):
        other = (z + d) % Z
        return pltpu.make_async_remote_copy(
            src_ref=counts_z.at[other], dst_ref=counts_z.at[other],
            send_sem=counts_send.at[d], recv_sem=counts_recv.at[other],
            device_id={"cell": cell_at(x, other, yh), "gene": gene}, device_id_type=MESH,
        )

    def totals_arrived(d):
        other = (z + d) % Z
        return pltpu.make_async_remote_copy(
            src_ref=totals_z.at[other], dst_ref=totals_z.at[other],
            send_sem=totals_send.at[d], recv_sem=totals_recv.at[other],
            device_id={"cell": cell_at(x, other, yh), "gene": gene}, device_id_type=MESH,
        )

    for d in range(1, Z):
        totals_copy(d).start()
    for d in range(1, Z):
        counts_copy(d).start()
    counts_z[z] = counts_ref[:, pl.ds(pl.multiple_of(z * GENES_Z, GENES_Z), GENES_Z)]
    totals_z[z] = totals_ref[...]

    lane = lax.broadcasted_iota(jnp.int32, (1, LANES), 1)

    def offset_of(slot):
        logs = jnp.log(totals_z[slot].astype(F32)) - LOG_SCALE
        return jnp.concatenate([logs[0:1], logs[1:2]], axis=1)

    loadings = loadings_ref[...].T
    for k in range(Z):
        loadings_t[k] = loadings[:, k * LANES : (k + 1) * LANES]
    factors = factors_ref[...].T
    factors_t[0] = factors[:, :LANES]
    factors_t[1] = factors[:, LANES:]
    left = left_stack(factors, offset_of(z))
    for k in range(Z):
        columns = slice(k * LANES, (k + 1) * LANES)
        rows = loadings_t[k]
        write_table(table1, columns, rows)
        expected = jnp.exp(predict(left, right_stack(rows)))
        weights1[:, columns] = expected.astype(BF16)
        residual1[:, columns] = (counts_ref[:, columns].astype(F32) - expected).astype(BF16)
    dims = (((1,), (1,)), ((), ()))
    curvature = lax.dot_general(
        table1[:TRIANGLE, :], weights1[...], dims, preferred_element_type=F32
    )
    gradient = lax.dot_general(
        table1[TRIANGLE:, :], residual1[...], dims, preferred_element_type=F32
    )
    for half in range(2):
        columns = slice(half * LANES, (half + 1) * LANES)
        sums1[half, :TRIANGLE, :] = curvature[:, columns]
        sums1[half, TRIANGLE:, :] = gradient[:, columns]

    core_copy = pltpu.make_async_remote_copy(
        src_ref=sums1.at[1 - core], dst_ref=core_in,
        send_sem=pair_send.at[0], recv_sem=pair_recv.at[0],
        device_id={"cell": cell, "gene": yl * 2 + 1 - core}, device_id_type=MESH,
    )
    core_copy.start()
    core_copy.wait_recv()
    middle = ROWS1 // 2
    top = sums1[core, :middle, :] + core_in[:middle, :]
    bottom = sums1[core, middle:, :] + core_in[middle:, :]
    low = lane < HALF
    first_pack = jnp.where(low, top, pltpu.roll(bottom, HALF, 1))
    second_pack = jnp.where(low, pltpu.roll(top, HALF, 1), bottom)
    yl_out[...] = jnp.where(yl == 0, second_pack, first_pack)
    yl_copy = pltpu.make_async_remote_copy(
        src_ref=yl_out, dst_ref=yl_in,
        send_sem=pair_send.at[1], recv_sem=pair_recv.at[1],
        device_id={"cell": cell, "gene": (1 - yl) * 2 + core}, device_id_type=MESH,
    )
    yl_copy.start()
    own_pack = jnp.where(yl == 0, first_pack, second_pack)
    yl_copy.wait_recv()
    total = own_pack + yl_in[...]
    packed[:middle, :] = total
    packed[middle:ROWS1, :] = pltpu.roll(total, HALF, 1)
    load_matrix(matrix, packed)
    old = factors_t[core]
    old = jnp.where(yl == 0, old, pltpu.roll(old, HALF, 1))
    right[...] = packed[TRIANGLE:ROWS1, :] - RIDGE * old
    new = old + solve(matrix, right, column, inverse)
    factor_slots[z, quarter] = jnp.where(low, new[:16], pltpu.roll(new[16:], HALF, 1))

    def factor_copy(k):
        other, step = k // 4, k % 4
        target = (z + other) % Z
        return pltpu.make_async_remote_copy(
            src_ref=factor_slots.at[z, quarter], dst_ref=factor_slots.at[z, quarter],
            send_sem=factor_send.at[k], recv_sem=factor_recv.at[z * 4 + quarter],
            device_id={"cell": cell_at(x, target, yh), "gene": (gene + step) % 4},
            device_id_type=MESH,
        )

    def factor_arrived(k):
        other, step = k // 4, k % 4
        source_z, source_gene = (z + other) % Z, (gene + step) % 4
        source_quarter = source_gene % 2 * 2 + source_gene // 2
        slot = factor_slots.at[source_z, source_quarter]
        return pltpu.make_async_remote_copy(
            src_ref=slot, dst_ref=slot,
            send_sem=factor_send.at[k], recv_sem=factor_recv.at[source_z * 4 + source_quarter],
            device_id={"cell": cell_at(x, source_z, yh), "gene": source_gene},
            device_id_type=MESH,
        )

    def run(action, first, last):
        def body(k, carry):
            action(k)
            return carry

        lax.fori_loop(first, last, body, 0)

    run(lambda k: factor_copy(k).start(), 1, 4 * Z)
    run(lambda k: factor_arrived(k).wait_recv(), 1, 4 * Z)
    for d in range(1, Z):
        totals_arrived(d).wait_recv()
    for d in range(1, Z):
        counts_arrived(d).wait_recv()

    def tile_of(slot, pair):
        first, second = factor_slots[slot, 2 * pair], factor_slots[slot, 2 * pair + 1]
        return jnp.concatenate(
            [
                jnp.where(low, first, pltpu.roll(second, HALF, 1)),
                jnp.where(low, pltpu.roll(first, HALF, 1), second),
            ],
            axis=0,
        )

    new_factors_ref[:LANES, :] = tile_of(z, 0).T
    new_factors_ref[LANES:, :] = tile_of(z, 1).T

    right2 = right_stack(loadings_t[z])
    deviance = jnp.zeros((8, LANES), F32)
    for k in range(Z):
        rows = jnp.concatenate([tile_of(k, 0), tile_of(k, 1)], axis=1)
        columns = slice(k * CELLS, (k + 1) * CELLS)
        write_table(table2, columns, rows)
        linear = predict(left_stack(rows, offset_of(k)), right2)
        expected = jnp.exp(linear)
        counts = counts_z[k].astype(F32)
        both2[columns, :LANES] = expected.astype(BF16)
        both2[columns, LANES:] = (counts - expected).astype(BF16)
        terms = 2.0 * (counts * (jnp.log(jnp.maximum(counts, 1.0)) - linear) - counts + expected)
        deviance = deviance + jnp.sum(terms.reshape(CELLS // 8, 8, LANES), axis=0)
    products = jnp.dot(table2[...], both2[...], preferred_element_type=F32)
    sums2[:TRIANGLE, :] = products[:TRIANGLE, :LANES]
    sums2[TRIANGLE:ROWS1, :] = products[TRIANGLE:, LANES:]
    sums2[ROWS1 : ROWS1 + 8, :] = deviance
    sums2[ROWS1 + 8 :, :] = jnp.zeros((ROWS2 - ROWS1 - 8, LANES), F32)

    block = lane // OWN_GENES
    for target in range(T):
        piece = jnp.zeros((PIECE2, LANES), F32)
        for k in range(T):
            rows = sums2[k * PIECE2 : (k + 1) * PIECE2, :]
            moved = rows if k == target else pltpu.roll(rows, (k - target) * OWN_GENES % LANES, 1)
            piece = jnp.where(block == k, moved, piece)
        piece_out[target] = piece

    def piece_copy(d):
        target = (t + d) % T
        return pltpu.make_async_remote_copy(
            src_ref=piece_out.at[target], dst_ref=piece_in.at[t],
            send_sem=piece_send.at[d], recv_sem=piece_recv.at[t],
            device_id={"cell": cell_at(target // YH, z, target % YH), "gene": gene},
            device_id_type=MESH,
        )

    def piece_arrived(d):
        source = (t + d) % T
        return pltpu.make_async_remote_copy(
            src_ref=piece_in.at[source], dst_ref=piece_in.at[source],
            send_sem=piece_send.at[d], recv_sem=piece_recv.at[source],
            device_id={"cell": cell_at(source // YH, z, source % YH), "gene": gene},
            device_id_type=MESH,
        )

    for d in range(1, T):
        piece_copy(d).start()
    piece_in[t] = piece_out[t]
    for d in range(1, T):
        piece_arrived(d).wait_recv()
    total = piece_in[0]
    for k in range(1, T):
        total = total + piece_in[k]
    for k in range(T):
        packed[k * PIECE2 : (k + 1) * PIECE2, :] = (
            total if k == 0 else pltpu.roll(total, LANES - k * OWN_GENES, 1)
        )
    load_matrix(matrix, packed)
    old = loadings_t[z]
    own = old
    for k in range(1, T):
        own = jnp.where(t == k, pltpu.roll(old, LANES - k * OWN_GENES, 1), own)
    right[...] = packed[TRIANGLE:ROWS1, :] - RIDGE * own
    new = own + solve(matrix, right, column, inverse)
    mean = jnp.sum(packed[ROWS1 : ROWS1 + 8, :], axis=0, keepdims=True) / (CELLS * CELL_DEVICES)
    message = jnp.where(block == 0, new[:8], 0.0)
    for k in range(1, 4):
        message = jnp.where(
            block == k, pltpu.roll(new[8 * k : 8 * k + 8], k * OWN_GENES, 1), message
        )
    mean = jnp.broadcast_to(mean, (8, LANES))
    final_out[...] = jnp.where(block == 4, pltpu.roll(mean, 4 * OWN_GENES, 1), message)

    def final_copy(d):
        return pltpu.make_async_remote_copy(
            src_ref=final_out, dst_ref=final_in.at[t, z],
            send_sem=final_send.at[d], recv_sem=final_recv.at[cell],
            device_id={"cell": (cell + d) % CELL_DEVICES, "gene": gene}, device_id_type=MESH,
        )

    def final_arrived(d):
        source = (cell + d) % CELL_DEVICES
        source_x, source_z, source_yh = source // (Z * YH), (source // YH) % Z, source % YH
        slot = final_in.at[source_x * YH + source_yh, source_z]
        return pltpu.make_async_remote_copy(
            src_ref=slot, dst_ref=slot,
            send_sem=final_send.at[d], recv_sem=final_recv.at[source],
            device_id={"cell": source, "gene": gene}, device_id_type=MESH,
        )

    run(lambda d: final_copy(d).start(), 1, CELL_DEVICES)
    final_in[t, z] = final_out[...]
    run(lambda d: final_arrived(d).wait_recv(), 1, CELL_DEVICES)
    for j in range(5):
        value = jnp.zeros((8 * Z, LANES), F32)
        for k in range(T):
            rows = final_in[k].reshape(8 * Z, LANES)
            moved = rows if k == j else pltpu.roll(rows, (k - j) * OWN_GENES % LANES, 1)
            value = jnp.where(block == k, moved, value)
        final_t[j] = value
    for k in range(Z):
        eight = slice(8 * k, 8 * k + 8)
        tile = jnp.concatenate([final_t[j, eight, :] for j in range(4)], axis=0)
        new_loadings_ref[k * LANES : (k + 1) * LANES, :] = tile.T
        deviance_ref[k : k + 1, :] = final_t[4, 8 * k : 8 * k + 1, :]

    for d in range(1, Z):
        counts_copy(d).wait_send()
        totals_copy(d).wait_send()
    core_copy.wait_send()
    yl_copy.wait_send()
    run(lambda k: factor_copy(k).wait_send(), 1, 4 * Z)
    for d in range(1, T):
        piece_copy(d).wait_send()
    run(lambda d: final_copy(d).wait_send(), 1, CELL_DEVICES)


def on_device(counts, totals, cell_factors, gene_loadings):
    vmem = pl.BlockSpec(memory_space=pltpu.VMEM)
    dma = pltpu.SemaphoreType.DMA
    new_factors, new_loadings, deviance = pl.pallas_call(
        kernel,
        out_shape=(
            jax.ShapeDtypeStruct((CELLS, WIDTH), F32),
            jax.ShapeDtypeStruct((GENES, WIDTH), F32),
            jax.ShapeDtypeStruct((Z, LANES), F32),
        ),
        in_specs=[vmem] * 4,
        out_specs=(vmem,) * 3,
        scratch_shapes=[
            pltpu.VMEM((Z, WIDTH, LANES), F32),
            pltpu.VMEM((2, WIDTH, LANES), F32),
            pltpu.VMEM((ROWS1, GENES), BF16),
            pltpu.VMEM((CELLS, GENES), BF16),
            pltpu.VMEM((CELLS, GENES), BF16),
            pltpu.VMEM((2, ROWS1, LANES), F32),
            pltpu.VMEM((ROWS1, LANES), F32),
            pltpu.VMEM((ROWS1 // 2, LANES), F32),
            pltpu.VMEM((ROWS1 // 2, LANES), F32),
            pltpu.VMEM((ROWS2, LANES), F32),
            pltpu.VMEM((WIDTH * WIDTH, LANES), F32),
            pltpu.VMEM((WIDTH, LANES), F32),
            pltpu.VMEM((WIDTH, LANES), F32),
            pltpu.VMEM((WIDTH, LANES), F32),
            pltpu.VMEM((Z, CELLS, LANES), jnp.int32),
            pltpu.VMEM((Z, 2, LANES), jnp.int32),
            pltpu.VMEM((Z, 4, 16, LANES), F32),
            pltpu.VMEM((ROWS1, Z * CELLS), BF16),
            pltpu.VMEM((Z * CELLS, 2 * LANES), BF16),
            pltpu.VMEM((ROWS2, LANES), F32),
            pltpu.VMEM((T, PIECE2, LANES), F32),
            pltpu.VMEM((T, PIECE2, LANES), F32),
            pltpu.VMEM((8, LANES), F32),
            pltpu.VMEM((T, Z, 8, LANES), F32),
            pltpu.VMEM((5, 8 * Z, LANES), F32),
            dma((Z,)), dma((Z,)), dma((Z,)), dma((Z,)), dma((2,)), dma((2,)),
            dma((4 * Z,)), dma((4 * Z,)), dma((T,)), dma((T,)),
            dma((CELL_DEVICES,)), dma((CELL_DEVICES,)),
        ],
        compiler_params=pltpu.CompilerParams(
            collective_id=0, has_side_effects=True, vmem_limit_bytes=48 * 1024 * 1024
        ),
        name="sweep",
    )(counts, totals.reshape(2, LANES), cell_factors, gene_loadings)
    return new_factors, new_loadings, deviance.reshape(GENES)


def solution(mesh):
    return jax.shard_map(
        on_device,
        mesh=mesh,
        in_specs=(P("cell", "gene"), P("cell"), P("cell", None), P("gene", None)),
        out_specs=(P("cell", None), P("gene", None), P("gene")),
        check_vma=False,
    )
```

time: 923 us -> 74.2 us (0.08); the launches traced: 907 us -> 73.7 us
  waiting for transfers between devices: 520 us -> 0 us
  blocking collectives: 190 us -> 0 us
  other arithmetic: 99.4 us -> 0 us
  Pallas kernels: 0 us -> 68.2 us
  local copies, waits for them, and re-layouts: 60.9 us -> 4.92 us
  between operations: 19.1 us -> 0.66 us
  starting transfers between devices: 9.67 us -> 0 us
    psum x1 -> x0, waiting for transfers between devices: 520 us -> none  [on_device(): lax.psum((gradient_part, curvature_part, deviance_part), 'cell')]
    psum x1 -> x0, blocking collectives: 185 us -> none  [on_device(): lax.psum((gradient_part, curvature_part, deviance_part), 'cell')]
    pallas_call x0 -> x1, Pallas kernels: none -> 68.2 us  [on_device(): pl.pallas_call(kernel, out_shape=(jax.ShapeDtypeStruct((CELLS, WIDTH), F3...]
    div x72 -> x0, other arithmetic: 36.3 us -> none  [the longest x59 15.5 us: newton_solve(): columns.append(mask * current / pivot[None, :])]
    unnamed x448 -> x11, local copies, waits for them, and re-layouts: 30.5 us -> 4.92 us
    reduce_sum x60 -> x0, other arithmetic: 21.6 us -> none  [newton_solve(): jnp.sum(stacked * stacked[:, column][:, None, :], axis=0)]
    slice x109 -> x0, local copies, waits for them, and re-layouts: 21.5 us -> none  [the longest x59 9.46 us: newton_solve(): stacked[:, column][:, None, :]]
    add x69 -> x0, other arithmetic: 17 us -> none  [the longest x64 15.2 us: newton_solve(): current + jnp.where(jnp.arange(width) == column, 1.0, 0.0).astype(jnp.flo...]
  transfers between devices with their start and end apart: 3 -> 0, of which waited for: 1 -> 0; matrix products, arithmetic and copies ran while one was open for 4% -> 0% of each run, Pallas kernels for 0% -> 0%
where the time goes in v1:
time: 74.2 us; the launch traced here: 73.7 us
  Pallas kernels  68.2 us (92%)
  local copies, waits for them, and re-layouts  4.92 us (7%)
    pallas_call x1, Pallas kernels, on_device(): pl.pallas_call(kernel, out_shape=(jax.ShapeDtypeStruct((CELLS, WIDTH), F3...  68.2 us
    unnamed x11, local copies, waits for them, and re-layouts  4.92 us

profile of v1, /device:TPU:8, one launch (start us, length us, event | category | flops | bytes accessed | tf_op | source)
XLA Modules:
  0.0 73.7 jit_solution(17993904675847371078)
XLA Ops:
  0.6 0.0 copy-start.2
  0.6 0.9 %copy.7.factors_ref = f32[256,32]{1,0:T(8,128)S(1)} copy(f32[256,32]{0,1:T(8,128)} %param.6) | data formatting | bytes 65536 | tf_op args[2]
  1.5 0.0 copy-done.2
  1.6 0.0 copy-start.1
  1.6 0.2 copy.8.loadings_ref
  1.8 0.5 copy-done.1
  2.2 0.0 copy-start
  2.2 1.2 %copy-done = s32[256,1024]{1,0:T(8,128)S(1)} copy-done((s32[256,1024]{1,0:T(8,128)S(1)}, s32[256,1024]{1,0:T(8,128)}, u32[]{:S(2)}) %copy-start) | copy-done | bytes 1048600
  3.5 68.2 %sweep.1 = (f32[256,32]{1,0:T(8,128)S(1)}, f32[1024,32]{1,0:T(8,128)S(1)}, f32[8,128]{1,0:T(8,128)S(1)}) custom-call(s32[256,1024]{1,0:T(8,128)S(1)} %copy-done, s32[2,128]{1,0:T(2,128)S(1)} %bitcast.3, f32[256,32]{1,0:T(8,128)S(1)} %copy.7.factors_ref, f32[1024,32]{1,0:T(8,128)S(1)} %copy.8.loadings_ref), custom_call_target="tpu_custom_call" | custom-call | tf_op jit(solution)/shard_map/sweep/pallas_call | solution.py:424
  71.6 0.7 copy.9
  72.3 0.8 %copy.10 = f32[1024,32]{0,1:T(8,128)} copy(f32[1024,32]{1,0:T(8,128)S(1)} %get-tuple-element.10) | data formatting | bytes 262144
  73.2 0.6 copy.12
Async XLA Ops:
  0.6 0.9 %copy-start.2 = (f32[1024,32]{0,1:T(8,128)S(1)}, f32[1024,32]{0,1:T(8,128)}, u32[]{:S(2)}) copy-start(f32[1024,32]{0,1:T(8,128)} %param.7) | copy-start | bytes 393220
  1.6 0.7 copy-start.1
  2.2 1.2 %copy-start = (s32[256,1024]{1,0:T(8,128)S(1)}, s32[256,1024]{1,0:T(8,128)}, u32[]{:S(2)}) copy-start(s32[256,1024]{1,0:T(8,128)} %counts_ref.1) | copy-start | bytes 3145732

commit v2 on v1

v2 whole, which is shorter than its diff:
```python
import math

import jax
import jax.numpy as jnp
from jax import lax
from jax.experimental import pallas as pl
from jax.experimental.pallas import tpu as pltpu
from jax.sharding import PartitionSpec as P

F32, BF16 = jnp.float32, jnp.bfloat16
MESH = pl.DeviceIdType.MESH

RIDGE = 1.0
DAMPING = 0.1
LOG_SCALE = math.log(5000.0)

WIDTH = 32
X, Z, YH = 4, 8, 2
CELL_DEVICES = X * Z * YH
T = X * YH
CELLS = 256
GENES = 1024
LANES = 128
GENES_Z = GENES // Z
OWN_GENES = GENES_Z // T
HALF = LANES // 2
CHUNK = 256
ORDER = (0, 1, 7, 2, 6, 3, 5, 4)

HEIGHT = [WIDTH - c // 8 * 8 for c in range(WIDTH)]
START = [sum(HEIGHT[:c]) for c in range(WIDTH)]
TRIANGLE = sum(HEIGHT)
ROWS1 = TRIANGLE + WIDTH
LOCAL = WIDTH + 8
ROWS2 = 704
PIECE2 = ROWS2 // T
MESSAGE = 5


def parts_of(value):
    high = value.astype(BF16).astype(F32)
    rest = value - high
    middle = rest.astype(BF16).astype(F32)
    return high, middle, rest - middle


def left_stack(factors, offset):
    high, middle, low = parts_of(factors)
    row = lax.broadcasted_iota(jnp.int32, (16, factors.shape[1]), 0)
    off_high, off_middle, off_low = parts_of(offset)
    extra = jnp.where(
        row == 0, off_high, jnp.where(row == 1, off_middle, jnp.where(row == 2, off_low, 0.0))
    )
    return jnp.concatenate([high, high, middle, middle, high, low, extra], axis=0).astype(BF16)


def right_stack(loadings):
    high, middle, low = parts_of(loadings)
    extra = jnp.ones((16, loadings.shape[1]), F32)
    return jnp.concatenate([high, middle, high, middle, low, high, extra], axis=0).astype(BF16)


def predict(left, right):
    return lax.dot_general(left, right, (((0,), (0,)), ((), ())), preferred_element_type=F32)


def write_table(table_ref, columns, rows):
    for c in range(0, WIDTH, 2):
        first = c // 8 * 8
        pair = jnp.concatenate(
            [rows[first:] * rows[c : c + 1], rows[first:] * rows[c + 1 : c + 2]], axis=0
        )
        table_ref[START[c] : START[c] + 2 * HEIGHT[c], columns] = pair.astype(BF16)
    table_ref[TRIANGLE : TRIANGLE + WIDTH, columns] = rows.astype(BF16)


def solve(matrix_ref, right_ref, column_ref, inverse_ref):
    for j in range(8, WIDTH):
        for block in range(j // 8):
            matrix_ref[WIDTH * j + 8 * block : WIDTH * j + 8 * block + 8, :] = matrix_ref[
                pl.ds(WIDTH * 8 * block + j, 8, stride=WIDTH), :
            ]
    diagonal = matrix_ref[pl.ds(0, WIDTH, stride=WIDTH + 1), :]
    shift = RIDGE + DAMPING * (jnp.sum(diagonal, axis=0, keepdims=True) / WIDTH)
    matrix_ref[pl.ds(0, WIDTH, stride=WIDTH + 1), :] = diagonal + shift
    row = lax.broadcasted_iota(jnp.int32, (WIDTH, LANES), 0)
    for group in range(WIDTH // 8):

        def step(c, carry):
            column = matrix_ref[pl.ds(pl.multiple_of(c * WIDTH, WIDTH), WIDTH), :]
            column_ref[...] = column
            inverse = 1.0 / column_ref[pl.ds(c, 1), :]
            inverse_ref[pl.ds(c, 1), :] = inverse
            scaled = jnp.where(row == c, 0.0, column * inverse)
            right_ref[...] = right_ref[...] - scaled * right_ref[pl.ds(c, 1), :]
            for j in range(8 * group, WIDTH):
                at = slice(WIDTH * j, WIDTH * j + WIDTH)
                matrix_ref[at, :] = matrix_ref[at, :] - scaled * column_ref[j : j + 1, :]
            return carry

        lax.fori_loop(8 * group, 8 * group + 8, step, 0)
    return right_ref[...] * inverse_ref[...]


def load_matrix(matrix_ref, packed_ref):
    for c in range(WIDTH):
        first = WIDTH - HEIGHT[c]
        matrix_ref[WIDTH * c + first : WIDTH * c + WIDTH, :] = packed_ref[
            START[c] : START[c] + HEIGHT[c], :
        ]


def swap_blocks(pieces, block):
    pieces = list(pieces)
    for bit in (1, 2, 4):
        keep = (block & bit) == 0
        for k in range(T):
            if k & bit == 0:
                first, second = pieces[k], pieces[k | bit]
                pieces[k] = jnp.where(keep, first, pltpu.roll(second, bit * OWN_GENES, 1))
                pieces[k | bit] = jnp.where(
                    keep, pltpu.roll(first, LANES - bit * OWN_GENES, 1), second
                )
    return pieces


def halves(tile, low):
    middle = tile.shape[0] // 2
    top, bottom = tile[:middle], tile[middle:]
    return (
        jnp.where(low, top, pltpu.roll(bottom, HALF, 1)),
        jnp.where(low, pltpu.roll(top, HALF, 1), bottom),
    )


def two_parts(value):
    high = value.astype(BF16)
    return high, (value - high.astype(F32)).astype(BF16)


def matmul_t(left, right):
    return lax.dot_general(left, right, (((1,), (1,)), ((), ())), preferred_element_type=F32)


def kernel(
    counts_hbm, totals_hbm, factors_hbm, loadings_hbm,
    new_factors_ref, new_loadings_ref, deviance_ref,
    counts_v, totals_v, totals_z, factors_v, loadings_v, mirror_v,
    right1, table1, high1, low1, counts_low, sums1, local1_out, local1_in, core_out, core_in,
    packed, matrix, right, column, inverse,
    factor_slots, local2_out, local2_in, table2, high2, low2, sums2, piece_out, piece_in,
    final_out, final_in, final_t,
    input_sem, totals_send, totals_recv, mirror_send, mirror_recv, local1_send, local1_recv, core_send, core_recv,
    factor_send, factor_recv, forward_send, local2_send, local2_recv, piece_send, piece_recv,
    final_send, final_recv,
):
    cell = lax.axis_index("cell")
    gene = lax.axis_index("gene")
    x, z, yh = cell // (Z * YH), (cell // YH) % Z, cell % YH
    yl, core = gene // 2, gene % 2
    t = x * YH + yh
    partner, mirror = yl * 2 + 1 - core, (1 - yl) * 2 + core

    def at(x_, z_, yh_, gene_):
        return {"cell": (x_ * Z + z_) * YH + yh_, "gene": gene_}

    def send(src, dst, send_sem, recv_sem, device):
        return pltpu.make_async_remote_copy(
            src_ref=src, dst_ref=dst, send_sem=send_sem, recv_sem=recv_sem,
            device_id=device, device_id_type=MESH,
        )

    def run(action, first, last):
        def body(k, carry):
            action(k)
            return carry

        lax.fori_loop(first, last, body, 0)

    barrier = pltpu.get_barrier_semaphore()

    def greet(device):
        pl.semaphore_signal(barrier, inc=1, device_id=device, device_id_type=MESH)

    for step in range(1, 4):
        greet(at(x, z, yh, (gene + step) % 4))
    for d in range(1, Z):
        greet(at(x, (z + d) % Z, yh, gene))
    for d in range(1, T):
        greet(at((t + d) % T // YH, z, (t + d) % YH, gene))
    inputs = [
        pltpu.make_async_copy(source, target, input_sem.at[k])
        for k, (source, target) in enumerate(
            [
                (loadings_hbm, loadings_v), (factors_hbm, factors_v),
                (totals_hbm, totals_v), (counts_hbm, counts_v),
            ]
        )
    ]
    for copy in inputs:
        copy.start()
    inputs[0].wait()
    pl.semaphore_wait(barrier, 3 + Z - 1 + T - 1)

    def mirror_copy(k):
        columns = slice(k * CHUNK, (k + 1) * CHUNK)
        return send(
            loadings_v.at[:, columns], mirror_v.at[:, columns],
            mirror_send.at[k], mirror_recv.at[k], at(x, z, yh, mirror),
        )

    def totals_copy(d):
        return send(
            totals_v, totals_z.at[z], totals_send.at[d], totals_recv.at[z],
            at(x, (z + d) % Z, yh, gene),
        )

    def totals_arrived(d):
        slot = totals_z.at[(z + d) % Z]
        return send(
            slot, slot, totals_send.at[d], totals_recv.at[(z + d) % Z],
            at(x, (z + d) % Z, yh, gene),
        )

    chunks = GENES // CHUNK
    for k in range(chunks):
        mirror_copy(k).start()
    for copy in inputs[1:]:
        copy.wait()

    for d in range(1, Z):
        totals_copy(d).start()
    totals_z[z] = totals_v[...]
    lane = lax.broadcasted_iota(jnp.int32, (1, LANES), 1)
    block = lane // OWN_GENES
    low = lane < HALF
    logs = jnp.log(totals_v[...].astype(F32)) - LOG_SCALE

    lanes_yl = pl.ds(pl.multiple_of(yl * LANES, LANES), LANES)
    old_factors = factors_v[:, lanes_yl]
    left1 = left_stack(old_factors, jnp.where(yl == 0, logs[0:1], logs[1:2]))

    def expect(rows, columns, keep):
        write_table(table1, columns, rows)
        stack = right_stack(rows)
        if keep:
            right1[:, columns] = stack
        high1[:, columns], low1[:, columns] = two_parts(jnp.exp(predict(left1, stack)))

    def contract(columns):
        return (
            matmul_t(table1[:, columns], high1[:, columns]),
            matmul_t(table1[TRIANGLE:, columns], low1[:, columns]),
        )

    for k in range(chunks):
        columns = slice(k * CHUNK, (k + 1) * CHUNK)
        expect(loadings_v[:, columns], columns, True)
    main, rest = contract(slice(0, GENES))
    sums1[:TRIANGLE, :] = main[:TRIANGLE]
    sums1[TRIANGLE:, :] = main[TRIANGLE:] + rest

    counts_low[...] = counts_v[...].astype(F32).astype(BF16)
    local1 = matmul_t(table1[TRIANGLE:, :GENES], counts_low[...])
    for pair in range(2):
        packs = halves(local1[:, pair * LANES : (pair + 1) * LANES], low)
        local1_out[2 * pair], local1_out[2 * pair + 1] = packs

    def local1_copy(step):
        target = (gene + step) % 4
        return send(
            local1_out.at[target], local1_in.at[gene],
            local1_send.at[step], local1_recv.at[gene], at(x, z, yh, target),
        )

    def local1_arrived(step):
        source = (gene + step) % 4
        slot = local1_in.at[source]
        return send(
            slot, slot, local1_send.at[step], local1_recv.at[source], at(x, z, yh, source)
        )

    for step in range(1, 4):
        local1_copy(step).start()
    local1_in[gene] = local1_out[gene]

    for part in range(2):
        for k in range(part * chunks // 2, (part + 1) * chunks // 2):
            mirror_copy(k).wait_recv()
            columns = slice(GENES + k * CHUNK, GENES + (k + 1) * CHUNK)
            expect(mirror_v[:, k * CHUNK : (k + 1) * CHUNK], columns, False)
        main, rest = contract(slice(GENES + part * GENES // 2, GENES + (part + 1) * GENES // 2))
        sums1[:TRIANGLE, :] = sums1[:TRIANGLE, :] + main[:TRIANGLE]
        sums1[TRIANGLE:, :] = sums1[TRIANGLE:, :] + main[TRIANGLE:] + rest

    first_pack, second_pack = halves(sums1[...], low)
    core_out[...] = jnp.where(core == 0, second_pack, first_pack)
    core_copy = send(
        core_out, core_in, core_send.at[0], core_recv.at[0], at(x, z, yh, partner)
    )
    core_copy.start()
    own_pack = jnp.where(core == 0, first_pack, second_pack)
    for step in range(1, 4):
        local1_arrived(step).wait_recv()
    counts_pack = local1_in[0] + local1_in[1] + local1_in[2] + local1_in[3]
    old = jnp.where(core == 0, old_factors, pltpu.roll(old_factors, HALF, 1))
    counts_part = jnp.concatenate([counts_pack, pltpu.roll(counts_pack, HALF, 1)], axis=0)
    core_copy.wait_recv()
    total = own_pack + core_in[...]
    middle = ROWS1 // 2
    packed[:middle, :] = total
    packed[middle:ROWS1, :] = pltpu.roll(total, HALF, 1)
    load_matrix(matrix, packed)
    right[...] = counts_part - packed[TRIANGLE:ROWS1, :] - RIDGE * old
    new = old + solve(matrix, right, column, inverse)
    factor_slots[z, gene] = jnp.where(low, new[:16], pltpu.roll(new[16:], HALF, 1))

    own_slot = factor_slots.at[z, gene]
    own_sem = factor_recv.at[z * 4 + gene]

    def near_copy(step):
        return send(
            own_slot, own_slot, factor_send.at[step], own_sem, at(x, z, yh, (gene + step) % 4)
        )

    def far_copy(d, side):
        return send(
            own_slot, own_slot, factor_send.at[4 + 2 * d + side], own_sem,
            at(x, (z + d) % Z, yh, side * 2 + core),
        )

    def slot_arrived(d, source):
        source_z = (z + d) % Z
        slot = factor_slots.at[source_z, source]
        return send(
            slot, slot, factor_send.at[0], factor_recv.at[source_z * 4 + source],
            at(x, z, yh, partner),
        )

    def forward_copy(d, side):
        source_z, source = (z + d) % Z, side * 2 + core
        slot = factor_slots.at[source_z, source]
        return send(
            slot, slot, forward_send.at[2 * d + side], factor_recv.at[source_z * 4 + source],
            at(x, z, yh, partner),
        )

    for step in range(1, 4):
        near_copy(step).start()
    for d in ORDER[1:]:
        for side in range(2):
            far_copy(d, side).start()

    def factors_of(d):
        slot = (z + d) % Z
        tiles = []
        for pair in range(2):
            first, second = factor_slots[slot, 2 * pair], factor_slots[slot, 2 * pair + 1]
            tiles.append(
                jnp.concatenate(
                    [
                        jnp.where(low, first, pltpu.roll(second, HALF, 1)),
                        jnp.where(low, pltpu.roll(first, HALF, 1), second),
                    ],
                    axis=0,
                )
            )
        return jnp.concatenate(tiles, axis=1)

    for step in range(1, 4):
        slot_arrived(0, (gene + step) % 4).wait_recv()
    rows = factors_of(0)
    new_factors_ref[...] = rows
    factors_low = rows.astype(BF16)
    left2 = left_stack(rows, jnp.concatenate([logs[0:1], logs[1:2]], axis=1))
    for k in range(Z):
        columns = slice(k * GENES_Z, (k + 1) * GENES_Z)
        local2_out[k, :WIDTH, :] = jnp.dot(
            factors_low, counts_low[:, columns], preferred_element_type=F32
        )
        counts = counts_v[:, columns].astype(F32)
        linear = predict(left2, right1[:, columns])
        terms = counts * (jnp.log(jnp.maximum(counts, 1.0)) - linear - 1.0)
        local2_out[k, WIDTH:, :] = jnp.sum(terms.reshape(CELLS // 8, 8, LANES), axis=0)

    def local2_copy(d):
        target = (z + d) % Z
        return send(
            local2_out.at[target], local2_in.at[z],
            local2_send.at[d], local2_recv.at[z], at(x, target, yh, gene),
        )

    def local2_arrived(d):
        source = (z + d) % Z
        slot = local2_in.at[source]
        return send(slot, slot, local2_send.at[d], local2_recv.at[source], at(x, source, yh, gene))

    for d in ORDER[1:]:
        local2_copy(d).start()
    local2_in[z] = local2_out[z]

    lanes_z = pl.ds(pl.multiple_of(z * GENES_Z, GENES_Z), GENES_Z)
    right2 = right1[:, lanes_z]
    expected_sum = jnp.zeros((8, LANES), F32)

    def offsets_of(d):
        logs_z = jnp.log(totals_z[(z + d) % Z].astype(F32)) - LOG_SCALE
        return jnp.concatenate([logs_z[0:1], logs_z[1:2]], axis=1)

    for part in range(2):
        for n in range(part * Z // 2, (part + 1) * Z // 2):
            if n > 0:
                for side in range(2):
                    slot_arrived(ORDER[n], side * 2 + core).wait_recv()
                    forward_copy(ORDER[n], side).start()
                for side in range(2):
                    slot_arrived(ORDER[n], side * 2 + 1 - core).wait_recv()
                totals_arrived(ORDER[n]).wait_recv()
            rows = factors_of(ORDER[n])
            columns = slice(n * CELLS, (n + 1) * CELLS)
            write_table(table2, columns, rows)
            expected = jnp.exp(predict(left_stack(rows, offsets_of(ORDER[n])), right2))
            high2[columns, :], low2[columns, :] = two_parts(expected)
            expected_sum = expected_sum + jnp.sum(
                expected.reshape(CELLS // 8, 8, LANES), axis=0
            )
        columns = slice(part * Z // 2 * CELLS, (part + 1) * Z // 2 * CELLS)
        main = jnp.dot(table2[:, columns], high2[columns, :], preferred_element_type=F32)
        rest = jnp.dot(table2[TRIANGLE:, columns], low2[columns, :], preferred_element_type=F32)
        if part == 0:
            sums2[:TRIANGLE, :] = main[:TRIANGLE]
            sums2[TRIANGLE:ROWS1, :] = -main[TRIANGLE:] - rest
        else:
            sums2[:TRIANGLE, :] = sums2[:TRIANGLE, :] + main[:TRIANGLE]
            sums2[TRIANGLE:ROWS1, :] = sums2[TRIANGLE:ROWS1, :] - main[TRIANGLE:] - rest
    run(lambda d: local2_arrived(d).wait_recv(), 1, Z)
    counts_part = local2_in[0]
    for k in range(1, Z):
        counts_part = counts_part + local2_in[k]
    sums2[TRIANGLE:ROWS1, :] = sums2[TRIANGLE:ROWS1, :] + counts_part[:WIDTH]
    sums2[ROWS1 : ROWS1 + 8, :] = counts_part[WIDTH:] + expected_sum
    sums2[ROWS1 + 8 :, :] = jnp.zeros((ROWS2 - ROWS1 - 8, LANES), F32)

    pieces = swap_blocks([sums2[k * PIECE2 : (k + 1) * PIECE2, :] for k in range(T)], block)
    for k in range(T):
        piece_out[k] = pieces[k]

    def piece_copy(d):
        target = (t + d) % T
        return send(
            piece_out.at[target], piece_in.at[t], piece_send.at[d], piece_recv.at[t],
            at(target // YH, z, target % YH, gene),
        )

    def piece_arrived(d):
        source = (t + d) % T
        slot = piece_in.at[source]
        return send(
            slot, slot, piece_send.at[d], piece_recv.at[source],
            at(source // YH, z, source % YH, gene),
        )

    for d in range(1, T):
        piece_copy(d).start()
    piece_in[t] = piece_out[t]
    for d in range(1, T):
        piece_arrived(d).wait_recv()
    total = piece_in[0]
    for k in range(1, T):
        total = total + piece_in[k]
    for k in range(T):
        packed[k * PIECE2 : (k + 1) * PIECE2, :] = (
            total if k == 0 else pltpu.roll(total, LANES - k * OWN_GENES, 1)
        )
    load_matrix(matrix, packed)
    old = loadings_v[:, lanes_z]
    own = old
    for k in range(1, T):
        own = jnp.where(t == k, pltpu.roll(old, LANES - k * OWN_GENES, 1), own)
    right[...] = packed[TRIANGLE:ROWS1, :] - RIDGE * own
    new = own + solve(matrix, right, column, inverse)
    mean = jnp.sum(packed[ROWS1 : ROWS1 + 8, :], axis=0, keepdims=True) * (
        2.0 / (CELLS * CELL_DEVICES)
    )

    message = new[:8]
    for k in range(1, 4):
        message = jnp.where(
            block == k, pltpu.roll(new[8 * k : 8 * k + 8], k * OWN_GENES, 1), message
        )
    row = lax.broadcasted_iota(jnp.int32, (8, LANES), 0)
    shifted = pltpu.roll(pltpu.roll(message, HALF, 1), 4, 0)
    message = jnp.where(low, message, shifted)
    final_out[...] = jnp.where(row < 4, message, jnp.broadcast_to(mean, (8, LANES)))

    used = slice(0, MESSAGE)

    def final_copy(d):
        target = (cell + d) % CELL_DEVICES
        return send(
            final_out.at[used], final_in.at[t, z, used],
            final_send.at[d], final_recv.at[cell], {"cell": target, "gene": gene},
        )

    def final_arrived(d):
        source = (cell + d) % CELL_DEVICES
        source_t = source // (Z * YH) * YH + source % YH
        slot = final_in.at[source_t, (source // YH) % Z, used]
        return send(
            slot, slot, final_send.at[d], final_recv.at[source], {"cell": source, "gene": gene}
        )

    run(lambda d: final_copy(d).start(), 1, CELL_DEVICES)
    final_in[t, z] = final_out[...]
    run(lambda d: final_arrived(d).wait_recv(), 1, CELL_DEVICES)
    row = lax.broadcasted_iota(jnp.int32, (8 * Z, LANES), 0) % 8
    slabs = []
    for k in range(T):
        rows = final_in[k].reshape(8 * Z, LANES)
        turned = pltpu.roll(rows, HALF, 1)
        slabs.append(
            jnp.where(low, jnp.where(row < 4, rows, pltpu.roll(turned, 4, 0)), turned)
        )
    slabs = swap_blocks(slabs, block)
    for j in range(5):
        final_t[j] = slabs[j]
    for k in range(Z):
        eight = slice(8 * k, 8 * k + 8)
        tile = jnp.concatenate([final_t[j, eight, :] for j in range(4)], axis=0)
        new_loadings_ref[:, k * LANES : (k + 1) * LANES] = tile
        deviance_ref[k : k + 1, :] = final_t[4, 8 * k + 4 : 8 * k + 5, :]

    for k in range(chunks):
        mirror_copy(k).wait_send()
    for step in range(1, 4):
        local1_copy(step).wait_send()
        near_copy(step).wait_send()
    core_copy.wait_send()
    for d in range(1, Z):
        for side in range(2):
            far_copy(d, side).wait_send()
            forward_copy(d, side).wait_send()
        local2_copy(d).wait_send()
        totals_copy(d).wait_send()
    for d in range(1, T):
        piece_copy(d).wait_send()
    run(lambda d: final_copy(d).wait_send(), 1, CELL_DEVICES)


def on_device(counts, totals, cell_factors, gene_loadings):
    hbm, vmem = pl.BlockSpec(memory_space=pltpu.HBM), pl.BlockSpec(memory_space=pltpu.VMEM)
    dma = pltpu.SemaphoreType.DMA
    new_factors, new_loadings, deviance = pl.pallas_call(
        kernel,
        out_shape=(
            jax.ShapeDtypeStruct((WIDTH, CELLS), F32),
            jax.ShapeDtypeStruct((WIDTH, GENES), F32),
            jax.ShapeDtypeStruct((Z, LANES), F32),
        ),
        in_specs=[hbm] * 4,
        out_specs=(vmem,) * 3,
        scratch_shapes=[
            pltpu.VMEM((CELLS, GENES), jnp.int32),
            pltpu.VMEM((2, LANES), jnp.int32),
            pltpu.VMEM((Z, 2, LANES), jnp.int32),
            pltpu.VMEM((WIDTH, CELLS), F32),
            pltpu.VMEM((WIDTH, GENES), F32),
            pltpu.VMEM((WIDTH, GENES), F32),
            pltpu.VMEM((6 * WIDTH + 16, GENES), BF16),
            pltpu.VMEM((ROWS1, 2 * GENES), BF16),
            pltpu.VMEM((LANES, 2 * GENES), BF16),
            pltpu.VMEM((LANES, 2 * GENES), BF16),
            pltpu.VMEM((CELLS, GENES), BF16),
            pltpu.VMEM((ROWS1, LANES), F32),
            pltpu.VMEM((4, 16, LANES), F32),
            pltpu.VMEM((4, 16, LANES), F32),
            pltpu.VMEM((ROWS1 // 2, LANES), F32),
            pltpu.VMEM((ROWS1 // 2, LANES), F32),
            pltpu.VMEM((ROWS2, LANES), F32),
            pltpu.VMEM((WIDTH * WIDTH, LANES), F32),
            pltpu.VMEM((WIDTH, LANES), F32),
            pltpu.VMEM((WIDTH, LANES), F32),
            pltpu.VMEM((WIDTH, LANES), F32),
            pltpu.VMEM((Z, 4, 16, LANES), F32),
            pltpu.VMEM((Z, LOCAL, LANES), F32),
            pltpu.VMEM((Z, LOCAL, LANES), F32),
            pltpu.VMEM((ROWS1, Z * CELLS), BF16),
            pltpu.VMEM((Z * CELLS, LANES), BF16),
            pltpu.VMEM((Z * CELLS, LANES), BF16),
            pltpu.VMEM((ROWS2, LANES), F32),
            pltpu.VMEM((T, PIECE2, LANES), F32),
            pltpu.VMEM((T, PIECE2, LANES), F32),
            pltpu.VMEM((8, LANES), F32),
            pltpu.VMEM((T, Z, 8, LANES), F32),
            pltpu.VMEM((5, 8 * Z, LANES), F32),
            dma((4,)), dma((Z,)), dma((Z,)), dma((4,)), dma((4,)), dma((4,)), dma((4,)),
            dma((1,)), dma((1,)), dma((4 + 2 * Z,)), dma((4 * Z,)), dma((2 * Z,)),
            dma((Z,)), dma((Z,)), dma((T,)), dma((T,)),
            dma((CELL_DEVICES,)), dma((CELL_DEVICES,)),
        ],
        compiler_params=pltpu.CompilerParams(
            collective_id=0, has_side_effects=True, vmem_limit_bytes=67043328
        ),
        name="sweep",
    )(counts, totals.reshape(2, LANES), cell_factors.T, gene_loadings.T)
    return new_factors.T, new_loadings.T, deviance.reshape(GENES)


def solution(mesh):
    return jax.shard_map(
        on_device,
        mesh=mesh,
        in_specs=(P("cell", "gene"), P("cell"), P("cell", None), P("gene", None)),
        out_specs=(P("cell", None), P("gene", None), P("gene")),
        check_vma=False,
    )
```

time: 74.2 us -> 58.1 us (0.78)
  Pallas kernels: 68.2 us -> 53.1 us
  local copies, waits for them, and re-layouts: 4.92 us -> 3.54 us
    pallas_call x1, Pallas kernels: 68.2 us -> 53.1 us  [on_device(): pl.pallas_call(kernel, out_shape=(jax.ShapeDtypeStruct((WIDTH, CELLS), F3...]
    unnamed x11 -> x5, local copies, waits for them, and re-layouts: 4.92 us -> 3.54 us
where the time goes in v2:
time: 58.1 us; the launch traced here: 57.2 us
  Pallas kernels  53.1 us (91%)
  local copies, waits for them, and re-layouts  3.54 us (6%)
  between operations  0.64 us (1%)
    pallas_call x1, Pallas kernels, on_device(): pl.pallas_call(kernel, out_shape=(jax.ShapeDtypeStruct((WIDTH, CELLS), F3...  53.1 us
    unnamed x5, local copies, waits for them, and re-layouts  3.54 us

profile of v2, /device:TPU:8, one launch (start us, length us, event | category | flops | bytes accessed | tf_op | source)
XLA Modules:
  0.0 57.2 jit_solution(2060350441595090040)
XLA Ops:
  0.6 53.1 %sweep.1 = (f32[32,256]{1,0:T(8,128)}, f32[32,1024]{1,0:T(8,128)}, f32[8,128]{1,0:T(8,128)}) custom-call(s32[256,1024]{1,0:T(8,128)} %counts_hbm.1, s32[2,128]{1,0:T(2,128)} %bitcast.11, f32[32,256]{1,0:T(8,128)} %bitcast.8, f32[32,1024]{1,0:T(8,128)} %bitcast.7), custom_call_target="tpu_custom_call" | custom-call | tf_op jit(solution)/shard_map/sweep/pallas_call | solution.py:553
  53.7 1.4 %copy.10 = f32[256,32]{0,1:T(8,128)} copy(f32[256,32]{0,1:T(8,128)} %bitcast.9) | data formatting | bytes 65536
  55.1 0.0 copy-start
  55.1 1.6 %copy.11 = f32[1024,32]{0,1:T(8,128)} copy(f32[1024,32]{0,1:T(8,128)} %bitcast.6) | data formatting | bytes 262144
  56.7 0.0 copy-done
  56.7 0.6 %copy.12 = f32[1024]{0:T(1024)} copy(f32[1024]{0:T(1024)S(1)} %bitcast.10) | data formatting | bytes 8192
Async XLA Ops:
  55.1 1.6 %copy-start = (f32[8,128]{1,0:T(8,128)S(1)}, f32[8,128]{1,0:T(8,128)}, u32[]{:S(2)}) copy-start(f32[8,128]{1,0:T(8,128)} %get-tuple-element.8) | copy-start | bytes 12292

commit v3 on v2

--- a/solution.py
+++ b/solution.py
@@ -84,22 +84,50 @@
     shift = RIDGE + DAMPING * (jnp.sum(diagonal, axis=0, keepdims=True) / WIDTH)
     matrix_ref[pl.ds(0, WIDTH, stride=WIDTH + 1), :] = diagonal + shift
     row = lax.broadcasted_iota(jnp.int32, (WIDTH, LANES), 0)
+
+    def enter(c, at, slot, first, second):
+        column_ref[slot, 0] = first
+        pivot = 1.0 / column_ref[slot, 0, pl.ds(at, 1), :]
+        inverse_ref[pl.ds(c, 1), :] = pivot
+        first_scaled = jnp.where(row == at, 0.0, first * pivot)
+        second = second - first_scaled * column_ref[slot, 0, pl.ds(at + 1, 1), :]
+        column_ref[slot, 1] = second
+        pivot = 1.0 / column_ref[slot, 1, pl.ds(at + 1, 1), :]
+        inverse_ref[pl.ds(c + 1, 1), :] = pivot
+        return first_scaled, jnp.where(row == at + 1, 0.0, second * pivot)
+
+    scaled = enter(0, 0, 0, matrix_ref[:WIDTH, :], matrix_ref[WIDTH : 2 * WIDTH, :])
     for group in range(WIDTH // 8):
 
-        def step(c, carry):
-            column = matrix_ref[pl.ds(pl.multiple_of(c * WIDTH, WIDTH), WIDTH), :]
-            column_ref[...] = column
-            inverse = 1.0 / column_ref[pl.ds(c, 1), :]
-            inverse_ref[pl.ds(c, 1), :] = inverse
-            scaled = jnp.where(row == c, 0.0, column * inverse)
-            right_ref[...] = right_ref[...] - scaled * right_ref[pl.ds(c, 1), :]
+        def step(pair, scaled):
+            first, second = scaled
+            c, slot = 2 * pair, pair % 2
+            after = jnp.minimum(c + 2, WIDTH - 2)
+
+            def reduced(value, j):
+                return (
+                    value
+                    - first * column_ref[slot, 0, pl.ds(j, 1), :]
+                    - second * column_ref[slot, 1, pl.ds(j, 1), :]
+                )
+
+            start = pl.multiple_of(after * WIDTH, WIDTH)
+            scaled_after = enter(
+                c + 2, after, 1 - slot,
+                reduced(matrix_ref[pl.ds(start, WIDTH), :], after),
+                reduced(matrix_ref[pl.ds(start + WIDTH, WIDTH), :], after + 1),
+            )
+            value = right_ref[...]
+            value = value - first * right_ref[pl.ds(c, 1), :]
+            right_ref[...] = value
+            right_ref[...] = value - second * right_ref[pl.ds(c + 1, 1), :]
             for j in range(8 * group, WIDTH):
                 at = slice(WIDTH * j, WIDTH * j + WIDTH)
-                matrix_ref[at, :] = matrix_ref[at, :] - scaled * column_ref[j : j + 1, :]
-            return carry
-
-        lax.fori_loop(8 * group, 8 * group + 8, step, 0)
-    return right_ref[...] * inverse_ref[...]
+                matrix_ref[at, :] = reduced(matrix_ref[at, :], j)
+            return scaled_after
+
+        scaled = lax.fori_loop(4 * group, 4 * group + 4, step, scaled)
+    return right_ref[...] * inverse_ref[:WIDTH, :]
 
 
 def load_matrix(matrix_ref, packed_ref):
@@ -144,14 +172,14 @@
 
 def kernel(
     counts_hbm, totals_hbm, factors_hbm, loadings_hbm,
-    new_factors_ref, new_loadings_ref, deviance_ref,
-    counts_v, totals_v, totals_z, factors_v, loadings_v, mirror_v,
+    factors_out_hbm, final_hbm,
+    factors_new, counts_v, totals_v, totals_z, factors_v, loadings_v, mirror_v,
     right1, table1, high1, low1, counts_low, sums1, local1_out, local1_in, core_out, core_in,
     packed, matrix, right, column, inverse,
-    factor_slots, local2_out, local2_in, table2, high2, low2, sums2, piece_out, piece_in,
-    final_out, final_in, final_t,
-    input_sem, totals_send, totals_recv, mirror_send, mirror_recv, local1_send, local1_recv, core_send, core_recv,
-    factor_send, factor_recv, forward_send, local2_send, local2_recv, piece_send, piece_recv,
+    factor_slots, local2_out, local2_in, local3_out, local3_in, table2, high2, low2, sums2, piece_out, piece_in,
+    final_out,
+    input_sem, output_sem, totals_send, totals_recv, mirror_send, mirror_recv, local1_send, local1_recv, core_send, core_recv,
+    factor_send, factor_recv, forward_send, local2_send, local2_recv, local3_send, local3_recv, piece_send, piece_recv,
     final_send, final_recv,
 ):
     cell = lax.axis_index("cell")
@@ -177,17 +205,6 @@
 
         lax.fori_loop(first, last, body, 0)
 
-    barrier = pltpu.get_barrier_semaphore()
-
-    def greet(device):
-        pl.semaphore_signal(barrier, inc=1, device_id=device, device_id_type=MESH)
-
-    for step in range(1, 4):
-        greet(at(x, z, yh, (gene + step) % 4))
-    for d in range(1, Z):
-        greet(at(x, (z + d) % Z, yh, gene))
-    for d in range(1, T):
-        greet(at((t + d) % T // YH, z, (t + d) % YH, gene))
     inputs = [
         pltpu.make_async_copy(source, target, input_sem.at[k])
         for k, (source, target) in enumerate(
@@ -199,6 +216,18 @@
     ]
     for copy in inputs:
         copy.start()
+
+    barrier = pltpu.get_barrier_semaphore()
+
+    def greet(device):
+        pl.semaphore_signal(barrier, inc=1, device_id=device, device_id_type=MESH)
+
+    for step in range(1, 4):
+        greet(at(x, z, yh, (gene + step) % 4))
+    for d in range(1, Z):
+        greet(at(x, (z + d) % Z, yh, gene))
+    for d in range(1, T):
+        greet(at((t + d) % T // YH, z, (t + d) % YH, gene))
     inputs[0].wait()
     pl.semaphore_wait(barrier, 3 + Z - 1 + T - 1)
 
@@ -367,78 +396,114 @@
             )
         return jnp.concatenate(tiles, axis=1)
 
+    def forward(first, last):
+        for n in range(first, last):
+            for side in range(2):
+                slot_arrived(ORDER[n], side * 2 + core).wait_recv()
+                forward_copy(ORDER[n], side).start()
+
     for step in range(1, 4):
         slot_arrived(0, (gene + step) % 4).wait_recv()
+    forward(1, 3)
     rows = factors_of(0)
-    new_factors_ref[...] = rows
+    factors_new[...] = rows
+    factors_out = pltpu.make_async_copy(factors_new, factors_out_hbm, output_sem.at[0])
+    factors_out.start()
     factors_low = rows.astype(BF16)
     left2 = left_stack(rows, jnp.concatenate([logs[0:1], logs[1:2]], axis=1))
+    locals2 = []
     for k in range(Z):
         columns = slice(k * GENES_Z, (k + 1) * GENES_Z)
-        local2_out[k, :WIDTH, :] = jnp.dot(
-            factors_low, counts_low[:, columns], preferred_element_type=F32
-        )
         counts = counts_v[:, columns].astype(F32)
         linear = predict(left2, right1[:, columns])
         terms = counts * (jnp.log(jnp.maximum(counts, 1.0)) - linear - 1.0)
-        local2_out[k, WIDTH:, :] = jnp.sum(terms.reshape(CELLS // 8, 8, LANES), axis=0)
+        locals2.append(
+            jnp.concatenate(
+                [
+                    jnp.dot(
+                        factors_low, counts_low[:, columns], preferred_element_type=F32
+                    ),
+                    jnp.sum(terms.reshape(CELLS // 8, 8, LANES), axis=0),
+                ],
+                axis=0,
+            )
+        )
+    locals2 = swap_blocks(locals2, block)
+    for k in range(T):
+        local2_out[k] = locals2[k]
 
     def local2_copy(d):
+        target = (t + d) % T
+        return send(
+            local2_out.at[target], local2_in.at[t], local2_send.at[d], local2_recv.at[t],
+            at(target // YH, z, target % YH, gene),
+        )
+
+    def local2_arrived(d):
+        source = (t + d) % T
+        slot = local2_in.at[source]
+        return send(
+            slot, slot, local2_send.at[d], local2_recv.at[source],
+            at(source // YH, z, source % YH, gene),
+        )
+
+    def local3_copy(d):
         target = (z + d) % Z
         return send(
-            local2_out.at[target], local2_in.at[z],
-            local2_send.at[d], local2_recv.at[z], at(x, target, yh, gene),
-        )
-
-    def local2_arrived(d):
+            local3_out.at[target], local3_in.at[z], local3_send.at[d], local3_recv.at[z],
+            at(x, target, yh, gene),
+        )
+
+    def local3_arrived(d):
         source = (z + d) % Z
-        slot = local2_in.at[source]
-        return send(slot, slot, local2_send.at[d], local2_recv.at[source], at(x, source, yh, gene))
-
-    for d in ORDER[1:]:
+        slot = local3_in.at[source]
+        return send(slot, slot, local3_send.at[d], local3_recv.at[source], at(x, source, yh, gene))
+
+    for d in range(1, T):
         local2_copy(d).start()
-    local2_in[z] = local2_out[z]
-
-    lanes_z = pl.ds(pl.multiple_of(z * GENES_Z, GENES_Z), GENES_Z)
-    right2 = right1[:, lanes_z]
-    expected_sum = jnp.zeros((8, LANES), F32)
+    local2_in[t] = local2_out[t]
+
+    right2 = right1[:, pl.ds(pl.multiple_of(z * GENES_Z, GENES_Z), GENES_Z)]
 
     def offsets_of(d):
         logs_z = jnp.log(totals_z[(z + d) % Z].astype(F32)) - LOG_SCALE
         return jnp.concatenate([logs_z[0:1], logs_z[1:2]], axis=1)
 
-    for part in range(2):
-        for n in range(part * Z // 2, (part + 1) * Z // 2):
-            if n > 0:
-                for side in range(2):
-                    slot_arrived(ORDER[n], side * 2 + core).wait_recv()
-                    forward_copy(ORDER[n], side).start()
-                for side in range(2):
-                    slot_arrived(ORDER[n], side * 2 + 1 - core).wait_recv()
-                totals_arrived(ORDER[n]).wait_recv()
-            rows = factors_of(ORDER[n])
-            columns = slice(n * CELLS, (n + 1) * CELLS)
-            write_table(table2, columns, rows)
-            expected = jnp.exp(predict(left_stack(rows, offsets_of(ORDER[n])), right2))
-            high2[columns, :], low2[columns, :] = two_parts(expected)
-            expected_sum = expected_sum + jnp.sum(
-                expected.reshape(CELLS // 8, 8, LANES), axis=0
-            )
-        columns = slice(part * Z // 2 * CELLS, (part + 1) * Z // 2 * CELLS)
+    def expect2(first, last):
+        for n in range(max(first, 1), last):
+            for side in range(2):
+                slot_arrived(ORDER[n], side * 2 + 1 - core).wait_recv()
+            totals_arrived(ORDER[n]).wait_recv()
+        rows = jnp.concatenate([factors_of(ORDER[n]) for n in range(first, last)], axis=1)
+        offsets = jnp.concatenate([offsets_of(ORDER[n]) for n in range(first, last)], axis=1)
+        columns = slice(first * CELLS, last * CELLS)
+        write_table(table2, columns, rows)
+        expected = jnp.exp(predict(left_stack(rows, offsets), right2))
+        high2[columns, :], low2[columns, :] = two_parts(expected)
+        return jnp.sum(expected.reshape((last - first) * CELLS // 8, 8, LANES), axis=0)
+
+    def contract2(first, last):
+        columns = slice(first * CELLS, last * CELLS)
         main = jnp.dot(table2[:, columns], high2[columns, :], preferred_element_type=F32)
         rest = jnp.dot(table2[TRIANGLE:, columns], low2[columns, :], preferred_element_type=F32)
-        if part == 0:
+        if first == 0:
             sums2[:TRIANGLE, :] = main[:TRIANGLE]
-            sums2[TRIANGLE:ROWS1, :] = -main[TRIANGLE:] - rest
+            sums2[TRIANGLE:ROWS1, :] = main[TRIANGLE:] + rest
         else:
             sums2[:TRIANGLE, :] = sums2[:TRIANGLE, :] + main[:TRIANGLE]
-            sums2[TRIANGLE:ROWS1, :] = sums2[TRIANGLE:ROWS1, :] - main[TRIANGLE:] - rest
-    run(lambda d: local2_arrived(d).wait_recv(), 1, Z)
-    counts_part = local2_in[0]
-    for k in range(1, Z):
-        counts_part = counts_part + local2_in[k]
-    sums2[TRIANGLE:ROWS1, :] = sums2[TRIANGLE:ROWS1, :] + counts_part[:WIDTH]
-    sums2[ROWS1 : ROWS1 + 8, :] = counts_part[WIDTH:] + expected_sum
+            sums2[TRIANGLE:ROWS1, :] = sums2[TRIANGLE:ROWS1, :] + main[TRIANGLE:] + rest
+
+    expected_sum = expect2(0, 1)
+    forward(3, 5)
+    expected_sum = expected_sum + expect2(1, 3)
+    forward(5, 7)
+    expected_sum = expected_sum + expect2(3, 5)
+    forward(7, 8)
+    contract2(0, 5)
+    expected_sum = expected_sum + expect2(5, 7)
+    expected_sum = expected_sum + expect2(7, 8)
+    contract2(5, 8)
+    sums2[ROWS1 : ROWS1 + 8, :] = expected_sum
     sums2[ROWS1 + 8 :, :] = jnp.zeros((ROWS2 - ROWS1 - 8, LANES), F32)
 
     pieces = swap_blocks([sums2[k * PIECE2 : (k + 1) * PIECE2, :] for k in range(T)], block)
@@ -463,6 +528,27 @@
     for d in range(1, T):
         piece_copy(d).start()
     piece_in[t] = piece_out[t]
+    for d in range(1, T):
+        local2_arrived(d).wait_recv()
+    counts_sum = local2_in[0]
+    for k in range(1, T):
+        counts_sum = counts_sum + local2_in[k]
+    zero = jnp.zeros((8, LANES), F32)
+    pieces = [counts_sum[8 * k : 8 * k + 8] for k in range(LOCAL // 8)]
+    pieces = swap_blocks(pieces + [zero] * (Z - LOCAL // 8), block)
+    for k in range(Z):
+        local3_out[k] = pieces[k]
+    for d in range(1, Z):
+        local3_copy(d).start()
+    local3_in[z] = local3_out[z]
+    for d in ORDER[1:]:
+        local3_arrived(d).wait_recv()
+    counts_sum = local3_in[0]
+    for k in range(1, Z):
+        counts_sum = counts_sum + local3_in[k]
+    counts_sum = [counts_sum] + [
+        pltpu.roll(counts_sum, LANES - k * OWN_GENES, 1) for k in range(1, LOCAL // 8)
+    ]
     for d in range(1, T):
         piece_arrived(d).wait_recv()
     total = piece_in[0]
@@ -473,13 +559,13 @@
             total if k == 0 else pltpu.roll(total, LANES - k * OWN_GENES, 1)
         )
     load_matrix(matrix, packed)
-    old = loadings_v[:, lanes_z]
+    old = loadings_v[:, pl.ds(pl.multiple_of(z * GENES_Z, GENES_Z), GENES_Z)]
     own = old
     for k in range(1, T):
         own = jnp.where(t == k, pltpu.roll(old, LANES - k * OWN_GENES, 1), own)
-    right[...] = packed[TRIANGLE:ROWS1, :] - RIDGE * own
+    right[...] = jnp.concatenate(counts_sum[:4], axis=0) - packed[TRIANGLE:ROWS1, :] - RIDGE * own
     new = own + solve(matrix, right, column, inverse)
-    mean = jnp.sum(packed[ROWS1 : ROWS1 + 8, :], axis=0, keepdims=True) * (
+    mean = jnp.sum(packed[ROWS1 : ROWS1 + 8, :] + counts_sum[4], axis=0, keepdims=True) * (
         2.0 / (CELLS * CELL_DEVICES)
     )
 
@@ -495,40 +581,36 @@
 
     used = slice(0, MESSAGE)
 
-    def final_copy(d):
-        target = (cell + d) % CELL_DEVICES
-        return send(
-            final_out.at[used], final_in.at[t, z, used],
-            final_send.at[d], final_recv.at[cell], {"cell": target, "gene": gene},
-        )
-
-    def final_arrived(d):
-        source = (cell + d) % CELL_DEVICES
-        source_t = source // (Z * YH) * YH + source % YH
-        slot = final_in.at[source_t, (source // YH) % Z, used]
-        return send(
-            slot, slot, final_send.at[d], final_recv.at[source], {"cell": source, "gene": gene}
-        )
-
-    run(lambda d: final_copy(d).start(), 1, CELL_DEVICES)
-    final_in[t, z] = final_out[...]
-    run(lambda d: final_arrived(d).wait_recv(), 1, CELL_DEVICES)
-    row = lax.broadcasted_iota(jnp.int32, (8 * Z, LANES), 0) % 8
-    slabs = []
-    for k in range(T):
-        rows = final_in[k].reshape(8 * Z, LANES)
-        turned = pltpu.roll(rows, HALF, 1)
-        slabs.append(
-            jnp.where(low, jnp.where(row < 4, rows, pltpu.roll(turned, 4, 0)), turned)
-        )
-    slabs = swap_blocks(slabs, block)
-    for j in range(5):
-        final_t[j] = slabs[j]
-    for k in range(Z):
-        eight = slice(8 * k, 8 * k + 8)
-        tile = jnp.concatenate([final_t[j, eight, :] for j in range(4)], axis=0)
-        new_loadings_ref[:, k * LANES : (k + 1) * LANES] = tile
-        deviance_ref[k : k + 1, :] = final_t[4, 8 * k + 4 : 8 * k + 5, :]
+    places = [(dx, dz, dy) for dx in range(X) for dz in range(Z) for dy in range(YH)]
+    places.sort(key=lambda p: -(min(p[0], X - p[0]) + min(p[1], Z - p[1]) + 2 * p[2]))
+    places = places[:-1]
+    xs = [(x + d) % X for d in range(X)]
+    zs = [(z + d) % Z for d in range(Z)]
+    ys = [(yh + d) % YH for d in range(YH)]
+
+    def cell_of(place):
+        return (xs[place[0]] * Z + zs[place[1]]) * YH + ys[place[2]]
+
+    def final_copy(k):
+        return send(
+            final_out.at[used], final_hbm.at[t, z, used], final_send.at[k], final_recv.at[cell],
+            {"cell": cell_of(places[k]), "gene": gene},
+        )
+
+    def final_arrived(k):
+        dx, dz, dy = places[k]
+        slot = final_hbm.at[xs[dx] * YH + ys[dy], zs[dz], used]
+        source = cell_of(places[k])
+        return send(
+            slot, slot, final_send.at[k], final_recv.at[source], {"cell": source, "gene": gene}
+        )
+
+    for k in range(len(places)):
+        final_copy(k).start()
+    own_final = pltpu.make_async_copy(
+        final_out.at[used], final_hbm.at[t, z, used], output_sem.at[1]
+    )
+    own_final.start()
 
     for k in range(chunks):
         mirror_copy(k).wait_send()
@@ -540,26 +622,52 @@
         for side in range(2):
             far_copy(d, side).wait_send()
             forward_copy(d, side).wait_send()
-        local2_copy(d).wait_send()
+        local3_copy(d).wait_send()
         totals_copy(d).wait_send()
     for d in range(1, T):
+        local2_copy(d).wait_send()
         piece_copy(d).wait_send()
-    run(lambda d: final_copy(d).wait_send(), 1, CELL_DEVICES)
+    factors_out.wait()
+    own_final.wait()
+    for k in range(len(places)):
+        final_copy(k).wait_send()
+    for k in reversed(range(len(places))):
+        final_arrived(k).wait_recv()
+
+
+def unpack(final_ref, factors_ref, new_factors_ref, new_loadings_ref, deviance_ref):
+    new_factors_ref[...] = factors_ref[...]
+    lane = lax.broadcasted_iota(jnp.int32, (1, LANES), 1)
+    row = lax.broadcasted_iota(jnp.int32, (8 * Z, LANES), 0) % 8
+    low = lane < HALF
+    slabs = []
+    for k in range(T):
+        rows = final_ref[k].reshape(8 * Z, LANES)
+        turned = pltpu.roll(rows, HALF, 1)
+        slabs.append(
+            jnp.where(low, jnp.where(row < 4, rows, pltpu.roll(turned, 4, 0)), turned)
+        )
+    slabs = swap_blocks(slabs, lane // OWN_GENES)
+    for k in range(Z):
+        eight = slice(8 * k, 8 * k + 8)
+        tile = jnp.concatenate([slabs[j][eight] for j in range(4)], axis=0)
+        new_loadings_ref[:, k * LANES : (k + 1) * LANES] = tile
+        deviance_ref[k : k + 1, :] = slabs[4][8 * k + 4 : 8 * k + 5]
 
 
 def on_device(counts, totals, cell_factors, gene_loadings):
     hbm, vmem = pl.BlockSpec(memory_space=pltpu.HBM), pl.BlockSpec(memory_space=pltpu.VMEM)
     dma = pltpu.SemaphoreType.DMA
-    new_factors, new_loadings, deviance = pl.pallas_call(
+    factors_new, final = pl.pallas_call(
         kernel,
         out_shape=(
             jax.ShapeDtypeStruct((WIDTH, CELLS), F32),
-            jax.ShapeDtypeStruct((WIDTH, GENES), F32),
-            jax.ShapeDtypeStruct((Z, LANES), F32),
+            jax.ShapeDtypeStruct((T, Z, 8, LANES), F32),
         ),
         in_specs=[hbm] * 4,
-        out_specs=(vmem,) * 3,
+        out_specs=(hbm,) * 2,
         scratch_shapes=[
+            pltpu.VMEM((WIDTH, CELLS), F32),
             pltpu.VMEM((CELLS, GENES), jnp.int32),
             pltpu.VMEM((2, LANES), jnp.int32),
             pltpu.VMEM((Z, 2, LANES), jnp.int32),
@@ -579,11 +687,13 @@
             pltpu.VMEM((ROWS2, LANES), F32),
             pltpu.VMEM((WIDTH * WIDTH, LANES), F32),
             pltpu.VMEM((WIDTH, LANES), F32),
-            pltpu.VMEM((WIDTH, LANES), F32),
-            pltpu.VMEM((WIDTH, LANES), F32),
+            pltpu.VMEM((2, 2, WIDTH, LANES), F32),
+            pltpu.VMEM((WIDTH + 8, LANES), F32),
             pltpu.VMEM((Z, 4, 16, LANES), F32),
-            pltpu.VMEM((Z, LOCAL, LANES), F32),
-            pltpu.VMEM((Z, LOCAL, LANES), F32),
+            pltpu.VMEM((T, LOCAL, LANES), F32),
+            pltpu.VMEM((T, LOCAL, LANES), F32),
+            pltpu.VMEM((Z, 8, LANES), F32),
+            pltpu.VMEM((Z, 8, LANES), F32),
             pltpu.VMEM((ROWS1, Z * CELLS), BF16),
             pltpu.VMEM((Z * CELLS, LANES), BF16),
             pltpu.VMEM((Z * CELLS, LANES), BF16),
@@ -591,11 +701,9 @@
             pltpu.VMEM((T, PIECE2, LANES), F32),
             pltpu.VMEM((T, PIECE2, LANES), F32),
             pltpu.VMEM((8, LANES), F32),
-            pltpu.VMEM((T, Z, 8, LANES), F32),
-            pltpu.VMEM((5, 8 * Z, LANES), F32),
-            dma((4,)), dma((Z,)), dma((Z,)), dma((4,)), dma((4,)), dma((4,)), dma((4,)),
+            dma((4,)), dma((2,)), dma((Z,)), dma((Z,)), dma((4,)), dma((4,)), dma((4,)), dma((4,)),
             dma((1,)), dma((1,)), dma((4 + 2 * Z,)), dma((4 * Z,)), dma((2 * Z,)),
-            dma((Z,)), dma((Z,)), dma((T,)), dma((T,)),
+            dma((T,)), dma((T,)), dma((Z,)), dma((Z,)), dma((T,)), dma((T,)),
             dma((CELL_DEVICES,)), dma((CELL_DEVICES,)),
         ],
         compiler_params=pltpu.CompilerParams(
@@ -603,6 +711,17 @@
         ),
         name="sweep",
     )(counts, totals.reshape(2, LANES), cell_factors.T, gene_loadings.T)
+    new_factors, new_loadings, deviance = pl.pallas_call(
+        unpack,
+        out_shape=(
+            jax.ShapeDtypeStruct((WIDTH, CELLS), F32),
+            jax.ShapeDtypeStruct((WIDTH, GENES), F32),
+            jax.ShapeDtypeStruct((Z, LANES), F32),
+        ),
+        in_specs=[vmem] * 2,
+        out_specs=(vmem,) * 3,
+        name="unpack",
+    )(final, factors_new)
     return new_factors.T, new_loadings.T, deviance.reshape(GENES)
 
 

time: 58.1 us -> 47.9 us (0.82)
  Pallas kernels: 53.1 us -> 46.7 us
  local copies, waits for them, and re-layouts: 3.54 us -> 0 us
    pallas_call x1, Pallas kernels: 53.1 us -> 44.8 us  [on_device(): pl.pallas_call(kernel, out_shape=(jax.ShapeDtypeStruct((WIDTH, CELLS), F3...]
    unnamed x5 -> x0, local copies, waits for them, and re-layouts: 3.54 us -> none
    pallas_call x0 -> x1, Pallas kernels: none -> 1.99 us  [on_device(): pl.pallas_call(unpack, out_shape=(jax.ShapeDtypeStruct((WIDTH, CELLS), F3...]
where the time goes in v3:
time: 47.9 us; the launch traced here: 47.4 us
  Pallas kernels  46.7 us (97%)
  between operations  0.64 us (1%)
    pallas_call x1, Pallas kernels, on_device(): pl.pallas_call(kernel, out_shape=(jax.ShapeDtypeStruct((WIDTH, CELLS), F3...  44.8 us
    pallas_call x1, Pallas kernels, on_device(): pl.pallas_call(unpack, out_shape=(jax.ShapeDtypeStruct((WIDTH, CELLS), F3...  1.99 us

profile of v3, /device:TPU:8, one launch (start us, length us, event | category | flops | bytes accessed | tf_op | source)
XLA Modules:
  0.0 47.4 jit_solution(8376157077740611282)
XLA Ops:
  0.6 44.8 %sweep.1 = (f32[32,256]{1,0:T(8,128)}, f32[8,8,8,128]{3,2,1,0:T(8,128)}) custom-call(s32[256,1024]{1,0:T(8,128)} %counts_hbm.1, s32[2,128]{1,0:T(2,128)} %bitcast.8, f32[32,256]{1,0:T(8,128)} %bitcast.7, f32[32,1024]{1,0:T(8,128)} %bitcast.6), custom_call_target="tpu_custom_call" | custom-call | tf_op jit(solution)/shard_map/sweep/pallas_call | solution.py:661
  45.4 2.0 %unpack.1 = (f32[32,256]{1,0:T(8,128)}, f32[32,1024]{1,0:T(8,128)}, f32[8,128]{1,0:T(8,128)}) custom-call(f32[8,8,8,128]{3,2,1,0:T(8,128)} %get-tuple-element.8.final_ref, f32[32,256]{1,0:T(8,128)} %get-tuple-element.9.factors_ref), custom_call_target="tpu_custom_call" | custom-call | tf_op jit(solution)/shard_map/unpack/pallas_call | solution.py:714

commit v4 on v3

--- a/solution.py
+++ b/solution.py
@@ -24,8 +24,10 @@
 GENES_Z = GENES // Z
 OWN_GENES = GENES_Z // T
 HALF = LANES // 2
-CHUNK = 256
+CHUNK = 128
 ORDER = (0, 1, 7, 2, 6, 3, 5, 4)
+FAR_FIRST = ORDER[:0:-1]
+PLANE = ((0, 0), (2, 1), (1, 1), (3, 1), (2, 0), (0, 1), (1, 0), (3, 0))
 
 HEIGHT = [WIDTH - c // 8 * 8 for c in range(WIDTH)]
 START = [sum(HEIGHT[:c]) for c in range(WIDTH)]
@@ -33,7 +35,6 @@
 ROWS1 = TRIANGLE + WIDTH
 LOCAL = WIDTH + 8
 ROWS2 = 704
-PIECE2 = ROWS2 // T
 MESSAGE = 5
 
 
@@ -74,7 +75,7 @@
     table_ref[TRIANGLE : TRIANGLE + WIDTH, columns] = rows.astype(BF16)
 
 
-def solve(matrix_ref, right_ref, column_ref, inverse_ref):
+def solve(matrix_ref, right_ref, first_ref, second_ref, inverse_ref):
     for j in range(8, WIDTH):
         for block in range(j // 8):
             matrix_ref[WIDTH * j + 8 * block : WIDTH * j + 8 * block + 8, :] = matrix_ref[
@@ -85,48 +86,51 @@
     matrix_ref[pl.ds(0, WIDTH, stride=WIDTH + 1), :] = diagonal + shift
     row = lax.broadcasted_iota(jnp.int32, (WIDTH, LANES), 0)
 
-    def enter(c, at, slot, first, second):
-        column_ref[slot, 0] = first
-        pivot = 1.0 / column_ref[slot, 0, pl.ds(at, 1), :]
+    def enter(c, at, column_ref, first, second):
+        column_ref[0] = first
+        pivot = 1.0 / column_ref[0, pl.ds(at, 1), :]
         inverse_ref[pl.ds(c, 1), :] = pivot
         first_scaled = jnp.where(row == at, 0.0, first * pivot)
-        second = second - first_scaled * column_ref[slot, 0, pl.ds(at + 1, 1), :]
-        column_ref[slot, 1] = second
-        pivot = 1.0 / column_ref[slot, 1, pl.ds(at + 1, 1), :]
+        second = second - first_scaled * column_ref[0, pl.ds(at + 1, 1), :]
+        column_ref[1] = second
+        pivot = 1.0 / column_ref[1, pl.ds(at + 1, 1), :]
         inverse_ref[pl.ds(c + 1, 1), :] = pivot
         return first_scaled, jnp.where(row == at + 1, 0.0, second * pivot)
 
-    scaled = enter(0, 0, 0, matrix_ref[:WIDTH, :], matrix_ref[WIDTH : 2 * WIDTH, :])
+    def advance(c, scaled, column_ref, column_next_ref, group):
+        first, second = scaled
+        after = jnp.minimum(c + 2, WIDTH - 2)
+
+        def reduced(value, j):
+            return (
+                value
+                - first * column_ref[0, pl.ds(j, 1), :]
+                - second * column_ref[1, pl.ds(j, 1), :]
+            )
+
+        start = pl.multiple_of(after * WIDTH, WIDTH)
+        scaled_after = enter(
+            c + 2, after, column_next_ref,
+            reduced(matrix_ref[pl.ds(start, WIDTH), :], after),
+            reduced(matrix_ref[pl.ds(start + WIDTH, WIDTH), :], after + 1),
+        )
+        value = right_ref[...]
+        value = value - first * right_ref[pl.ds(c, 1), :]
+        right_ref[...] = value
+        right_ref[...] = value - second * right_ref[pl.ds(c + 1, 1), :]
+        for j in range(8 * group, WIDTH):
+            at = slice(WIDTH * j, WIDTH * j + WIDTH)
+            matrix_ref[at, :] = reduced(matrix_ref[at, :], j)
+        return scaled_after
+
+    scaled = enter(0, 0, first_ref, matrix_ref[:WIDTH, :], matrix_ref[WIDTH : 2 * WIDTH, :])
     for group in range(WIDTH // 8):
 
-        def step(pair, scaled):
-            first, second = scaled
-            c, slot = 2 * pair, pair % 2
-            after = jnp.minimum(c + 2, WIDTH - 2)
-
-            def reduced(value, j):
-                return (
-                    value
-                    - first * column_ref[slot, 0, pl.ds(j, 1), :]
-                    - second * column_ref[slot, 1, pl.ds(j, 1), :]
-                )
-
-            start = pl.multiple_of(after * WIDTH, WIDTH)
-            scaled_after = enter(
-                c + 2, after, 1 - slot,
-                reduced(matrix_ref[pl.ds(start, WIDTH), :], after),
-                reduced(matrix_ref[pl.ds(start + WIDTH, WIDTH), :], after + 1),
-            )
-            value = right_ref[...]
-            value = value - first * right_ref[pl.ds(c, 1), :]
-            right_ref[...] = value
-            right_ref[...] = value - second * right_ref[pl.ds(c + 1, 1), :]
-            for j in range(8 * group, WIDTH):
-                at = slice(WIDTH * j, WIDTH * j + WIDTH)
-                matrix_ref[at, :] = reduced(matrix_ref[at, :], j)
-            return scaled_after
-
-        scaled = lax.fori_loop(4 * group, 4 * group + 4, step, scaled)
+        def step(quad, scaled):
+            scaled = advance(4 * quad, scaled, first_ref, second_ref, group)
+            return advance(4 * quad + 2, scaled, second_ref, first_ref, group)
+
+        scaled = lax.fori_loop(2 * group, 2 * group + 2, step, scaled)
     return right_ref[...] * inverse_ref[:WIDTH, :]
 
 
@@ -175,10 +179,11 @@
     factors_out_hbm, final_hbm,
     factors_new, counts_v, totals_v, totals_z, factors_v, loadings_v, mirror_v,
     right1, table1, high1, low1, counts_low, sums1, local1_out, local1_in, core_out, core_in,
-    packed, matrix, right, column, inverse,
-    factor_slots, local2_out, local2_in, local3_out, local3_in, table2, high2, low2, sums2, piece_out, piece_in,
+    packed, matrix, right, column_a, column_b, inverse,
+    factor_slots, local2_out, local2_in, local3_out, local3_in, table2, high2, low2, sums2, bases,
+    piece_out_a, piece_in_a, piece_out_b, piece_in_b,
     final_out,
-    input_sem, output_sem, totals_send, totals_recv, mirror_send, mirror_recv, local1_send, local1_recv, core_send, core_recv,
+    rounds, input_sem, output_sem, totals_send, totals_recv, mirror_send, mirror_recv, local1_send, local1_recv, core_send, core_recv,
     factor_send, factor_recv, forward_send, local2_send, local2_recv, local3_send, local3_recv, piece_send, piece_recv,
     final_send, final_recv,
 ):
@@ -192,6 +197,9 @@
     def at(x_, z_, yh_, gene_):
         return {"cell": (x_ * Z + z_) * YH + yh_, "gene": gene_}
 
+    def plane(k):
+        return (x + PLANE[k][0]) % X * YH + (yh + PLANE[k][1]) % YH
+
     def send(src, dst, send_sem, recv_sem, device):
         return pltpu.make_async_remote_copy(
             src_ref=src, dst_ref=dst, send_sem=send_sem, recv_sem=recv_sem,
@@ -224,18 +232,37 @@
 
     for step in range(1, 4):
         greet(at(x, z, yh, (gene + step) % 4))
-    for d in range(1, Z):
+    greet(at(x, z, 1 - yh, mirror))
+    greet(at(x, z, 1 - yh, gene))
+    steps_z, steps_x = (1, Z - 1, 2, Z - 2), (1, X - 1, 2)
+    for d in steps_z:
         greet(at(x, (z + d) % Z, yh, gene))
-    for d in range(1, T):
-        greet(at((t + d) % T // YH, z, (t + d) % YH, gene))
+    for d in steps_x:
+        greet(at((x + d) % X, z, yh, gene))
+
+    def tell(first, devices):
+        for k, device in enumerate(devices):
+            pl.semaphore_signal(
+                rounds.at[first + k], inc=1, device_id=device, device_id_type=MESH
+            )
+
+    def told(first, last):
+        for k in range(first, last):
+            pl.semaphore_wait(rounds.at[k], 1)
+
     inputs[0].wait()
-    pl.semaphore_wait(barrier, 3 + Z - 1 + T - 1)
+    pl.semaphore_wait(barrier, 12)
+    tell(0, [at(x, (z + d) % Z, yh, gene) for d in steps_z])
+    tell(6, [at((x + d) % X, z, yh, gene) for d in steps_x])
+
+    chunks = GENES // CHUNK
 
     def mirror_copy(k):
         columns = slice(k * CHUNK, (k + 1) * CHUNK)
         return send(
             loadings_v.at[:, columns], mirror_v.at[:, columns],
-            mirror_send.at[k], mirror_recv.at[k], at(x, z, yh, mirror),
+            mirror_send.at[k], mirror_recv.at[k],
+            at(x, z, yh if k < chunks // 2 else 1 - yh, mirror),
         )
 
     def totals_copy(d):
@@ -251,14 +278,12 @@
             at(x, (z + d) % Z, yh, gene),
         )
 
-    chunks = GENES // CHUNK
-    for k in range(chunks):
+    arrival = [k // 2 + k % 2 * (chunks // 2) for k in range(chunks)]
+    for k in arrival:
         mirror_copy(k).start()
     for copy in inputs[1:]:
         copy.wait()
 
-    for d in range(1, Z):
-        totals_copy(d).start()
     totals_z[z] = totals_v[...]
     lane = lax.broadcasted_iota(jnp.int32, (1, LANES), 1)
     block = lane // OWN_GENES
@@ -282,8 +307,8 @@
             matmul_t(table1[TRIANGLE:, columns], low1[:, columns]),
         )
 
-    for k in range(chunks):
-        columns = slice(k * CHUNK, (k + 1) * CHUNK)
+    for k in range(0, chunks, 2):
+        columns = slice(k * CHUNK, (k + 2) * CHUNK)
         expect(loadings_v[:, columns], columns, True)
     main, rest = contract(slice(0, GENES))
     sums1[:TRIANGLE, :] = main[:TRIANGLE]
@@ -313,12 +338,15 @@
         local1_copy(step).start()
     local1_in[gene] = local1_out[gene]
 
-    for part in range(2):
-        for k in range(part * chunks // 2, (part + 1) * chunks // 2):
-            mirror_copy(k).wait_recv()
-            columns = slice(GENES + k * CHUNK, GENES + (k + 1) * CHUNK)
-            expect(mirror_v[:, k * CHUNK : (k + 1) * CHUNK], columns, False)
-        main, rest = contract(slice(GENES + part * GENES // 2, GENES + (part + 1) * GENES // 2))
+    for k in range(0, chunks, 2):
+        for n in range(k, k + 2):
+            mirror_copy(arrival[n]).wait_recv()
+        rows = jnp.concatenate(
+            [mirror_v[:, n * CHUNK : (n + 1) * CHUNK] for n in arrival[k : k + 2]], axis=1
+        )
+        columns = slice(GENES + k * CHUNK, GENES + (k + 2) * CHUNK)
+        expect(rows, columns, False)
+        main, rest = contract(columns)
         sums1[:TRIANGLE, :] = sums1[:TRIANGLE, :] + main[:TRIANGLE]
         sums1[TRIANGLE:, :] = sums1[TRIANGLE:, :] + main[TRIANGLE:] + rest
 
@@ -328,6 +356,8 @@
         core_out, core_in, core_send.at[0], core_recv.at[0], at(x, z, yh, partner)
     )
     core_copy.start()
+    told(0, 4)
+    tell(4, [at(x, (z + d) % Z, yh, gene) for d in steps_z[2:]])
     own_pack = jnp.where(core == 0, first_pack, second_pack)
     for step in range(1, 4):
         local1_arrived(step).wait_recv()
@@ -341,7 +371,7 @@
     packed[middle:ROWS1, :] = pltpu.roll(total, HALF, 1)
     load_matrix(matrix, packed)
     right[...] = counts_part - packed[TRIANGLE:ROWS1, :] - RIDGE * old
-    new = old + solve(matrix, right, column, inverse)
+    new = old + solve(matrix, right, column_a, column_b, inverse)
     factor_slots[z, gene] = jnp.where(low, new[:16], pltpu.roll(new[16:], HALF, 1))
 
     own_slot = factor_slots.at[z, gene]
@@ -376,9 +406,12 @@
 
     for step in range(1, 4):
         near_copy(step).start()
-    for d in ORDER[1:]:
+    told(4, 6)
+    for d in FAR_FIRST:
         for side in range(2):
             far_copy(d, side).start()
+    for d in FAR_FIRST:
+        totals_copy(d).start()
 
     def factors_of(d):
         slot = (z + d) % Z
@@ -402,45 +435,49 @@
                 slot_arrived(ORDER[n], side * 2 + core).wait_recv()
                 forward_copy(ORDER[n], side).start()
 
+    for k in range(Z):
+        counts = counts_v[:, k * GENES_Z : (k + 1) * GENES_Z].astype(F32)
+        terms = counts * (jnp.log(jnp.maximum(counts, 1.0)) - 1.0)
+        bases[k] = jnp.sum(terms.reshape(CELLS // 8, 8, LANES), axis=0)
     for step in range(1, 4):
         slot_arrived(0, (gene + step) % 4).wait_recv()
-    forward(1, 3)
     rows = factors_of(0)
     factors_new[...] = rows
     factors_out = pltpu.make_async_copy(factors_new, factors_out_hbm, output_sem.at[0])
     factors_out.start()
-    factors_low = rows.astype(BF16)
-    left2 = left_stack(rows, jnp.concatenate([logs[0:1], logs[1:2]], axis=1))
+    factor_parts = parts_of(rows)
+    offset_parts = parts_of(jnp.concatenate([logs[0:1], logs[1:2]], axis=1))
+    row = lax.broadcasted_iota(jnp.int32, (16, CELLS), 0)
+    extra = jnp.zeros((16, CELLS), F32)
+    for k in range(3):
+        extra = jnp.where(row == k, offset_parts[k], extra)
+    left2 = jnp.concatenate([*factor_parts, extra], axis=0).astype(BF16)
+    row = lax.broadcasted_iota(jnp.int32, (8, LANES), 0)
     locals2 = []
     for k in range(Z):
         columns = slice(k * GENES_Z, (k + 1) * GENES_Z)
-        counts = counts_v[:, columns].astype(F32)
-        linear = predict(left2, right1[:, columns])
-        terms = counts * (jnp.log(jnp.maximum(counts, 1.0)) - linear - 1.0)
-        locals2.append(
-            jnp.concatenate(
-                [
-                    jnp.dot(
-                        factors_low, counts_low[:, columns], preferred_element_type=F32
-                    ),
-                    jnp.sum(terms.reshape(CELLS // 8, 8, LANES), axis=0),
-                ],
-                axis=0,
-            )
-        )
+        product = jnp.dot(left2, counts_low[:, columns], preferred_element_type=F32)
+        gradient = product[:WIDTH]
+        weighted = loadings_v[:, columns] * (
+            gradient + product[WIDTH : 2 * WIDTH] + product[2 * WIDTH : 3 * WIDTH]
+        )
+        linear = jnp.where(row < 3, product[3 * WIDTH : 3 * WIDTH + 8], 0.0)
+        for n in range(WIDTH // 8):
+            linear = linear + weighted[8 * n : 8 * n + 8]
+        locals2.append(jnp.concatenate([gradient, bases[k] - linear], axis=0))
     locals2 = swap_blocks(locals2, block)
     for k in range(T):
         local2_out[k] = locals2[k]
 
     def local2_copy(d):
-        target = (t + d) % T
+        target = plane(d)
         return send(
             local2_out.at[target], local2_in.at[t], local2_send.at[d], local2_recv.at[t],
             at(target // YH, z, target % YH, gene),
         )
 
     def local2_arrived(d):
-        source = (t + d) % T
+        source = plane(d)
         slot = local2_in.at[source]
         return send(
             slot, slot, local2_send.at[d], local2_recv.at[source],
@@ -459,6 +496,7 @@
         slot = local3_in.at[source]
         return send(slot, slot, local3_send.at[d], local3_recv.at[source], at(x, source, yh, gene))
 
+    told(6, 9)
     for d in range(1, T):
         local2_copy(d).start()
     local2_in[t] = local2_out[t]
@@ -469,11 +507,13 @@
         logs_z = jnp.log(totals_z[(z + d) % Z].astype(F32)) - LOG_SCALE
         return jnp.concatenate([logs_z[0:1], logs_z[1:2]], axis=1)
 
-    def expect2(first, last):
-        for n in range(max(first, 1), last):
+    def wait2(first, last):
+        for n in range(first, last):
             for side in range(2):
                 slot_arrived(ORDER[n], side * 2 + 1 - core).wait_recv()
             totals_arrived(ORDER[n]).wait_recv()
+
+    def expect2(first, last):
         rows = jnp.concatenate([factors_of(ORDER[n]) for n in range(first, last)], axis=1)
         offsets = jnp.concatenate([offsets_of(ORDER[n]) for n in range(first, last)], axis=1)
         columns = slice(first * CELLS, last * CELLS)
@@ -482,52 +522,62 @@
         high2[columns, :], low2[columns, :] = two_parts(expected)
         return jnp.sum(expected.reshape((last - first) * CELLS // 8, 8, LANES), axis=0)
 
-    def contract2(first, last):
+    def contract2(first, last, top, bottom):
         columns = slice(first * CELLS, last * CELLS)
-        main = jnp.dot(table2[:, columns], high2[columns, :], preferred_element_type=F32)
-        rest = jnp.dot(table2[TRIANGLE:, columns], low2[columns, :], preferred_element_type=F32)
-        if first == 0:
-            sums2[:TRIANGLE, :] = main[:TRIANGLE]
-            sums2[TRIANGLE:ROWS1, :] = main[TRIANGLE:] + rest
-        else:
-            sums2[:TRIANGLE, :] = sums2[:TRIANGLE, :] + main[:TRIANGLE]
-            sums2[TRIANGLE:ROWS1, :] = sums2[TRIANGLE:ROWS1, :] + main[TRIANGLE:] + rest
-
+        rows = slice(top, bottom)
+        main = jnp.dot(table2[rows, columns], high2[columns, :], preferred_element_type=F32)
+        sums2[rows, :] = main if first == 0 else sums2[rows, :] + main
+        if bottom == ROWS1:
+            sums2[TRIANGLE:ROWS1, :] = sums2[TRIANGLE:ROWS1, :] + jnp.dot(
+                table2[TRIANGLE:, columns], low2[columns, :], preferred_element_type=F32
+            )
+
+    forward(1, 3)
     expected_sum = expect2(0, 1)
     forward(3, 5)
+    wait2(1, 3)
     expected_sum = expected_sum + expect2(1, 3)
     forward(5, 7)
+    contract2(0, 3, 0, ROWS1)
+    forward(7, 8)
+    wait2(3, 5)
     expected_sum = expected_sum + expect2(3, 5)
-    forward(7, 8)
-    contract2(0, 5)
+    wait2(5, 7)
+    contract2(3, 5, 0, ROWS1)
     expected_sum = expected_sum + expect2(5, 7)
+    wait2(7, 8)
+    contract2(5, 7, 0, ROWS1)
     expected_sum = expected_sum + expect2(7, 8)
-    contract2(5, 8)
     sums2[ROWS1 : ROWS1 + 8, :] = expected_sum
     sums2[ROWS1 + 8 :, :] = jnp.zeros((ROWS2 - ROWS1 - 8, LANES), F32)
 
-    pieces = swap_blocks([sums2[k * PIECE2 : (k + 1) * PIECE2, :] for k in range(T)], block)
-    for k in range(T):
-        piece_out[k] = pieces[k]
-
-    def piece_copy(d):
-        target = (t + d) % T
-        return send(
-            piece_out.at[target], piece_in.at[t], piece_send.at[d], piece_recv.at[t],
+    parts = ((0, 48, piece_out_a, piece_in_a), (T * 48, 40, piece_out_b, piece_in_b))
+
+    def piece_copy(part, d):
+        target = plane(d)
+        return send(
+            parts[part][2].at[target], parts[part][3].at[t],
+            piece_send.at[part * T + d], piece_recv.at[part * T + t],
             at(target // YH, z, target % YH, gene),
         )
 
-    def piece_arrived(d):
-        source = (t + d) % T
-        slot = piece_in.at[source]
-        return send(
-            slot, slot, piece_send.at[d], piece_recv.at[source],
+    def piece_arrived(part, d):
+        source = plane(d)
+        slot = parts[part][3].at[source]
+        return send(
+            slot, slot, piece_send.at[part * T + d], piece_recv.at[part * T + source],
             at(source // YH, z, source % YH, gene),
         )
 
-    for d in range(1, T):
-        piece_copy(d).start()
-    piece_in[t] = piece_out[t]
+    for part, (top, height, out_ref, in_ref) in enumerate(parts):
+        contract2(7, 8, top, min(top + T * height, ROWS1))
+        rows = [sums2[top + k * height : top + (k + 1) * height, :] for k in range(T)]
+        rows = swap_blocks(rows, block)
+        for k in range(T):
+            out_ref[k] = rows[k]
+        for d in range(1, T):
+            piece_copy(part, d).start()
+        in_ref[t] = out_ref[t]
     for d in range(1, T):
         local2_arrived(d).wait_recv()
     counts_sum = local2_in[0]
@@ -538,7 +588,7 @@
     pieces = swap_blocks(pieces + [zero] * (Z - LOCAL // 8), block)
     for k in range(Z):
         local3_out[k] = pieces[k]
-    for d in range(1, Z):
+    for d in FAR_FIRST:
         local3_copy(d).start()
     local3_in[z] = local3_out[z]
     for d in ORDER[1:]:
@@ -549,22 +599,23 @@
     counts_sum = [counts_sum] + [
         pltpu.roll(counts_sum, LANES - k * OWN_GENES, 1) for k in range(1, LOCAL // 8)
     ]
-    for d in range(1, T):
-        piece_arrived(d).wait_recv()
-    total = piece_in[0]
-    for k in range(1, T):
-        total = total + piece_in[k]
-    for k in range(T):
-        packed[k * PIECE2 : (k + 1) * PIECE2, :] = (
-            total if k == 0 else pltpu.roll(total, LANES - k * OWN_GENES, 1)
-        )
+    for part, (top, height, out_ref, in_ref) in enumerate(parts):
+        for d in range(1, T):
+            piece_arrived(part, d).wait_recv()
+        total = in_ref[0]
+        for k in range(1, T):
+            total = total + in_ref[k]
+        for k in range(T):
+            packed[top + k * height : top + (k + 1) * height, :] = (
+                total if k == 0 else pltpu.roll(total, LANES - k * OWN_GENES, 1)
+            )
     load_matrix(matrix, packed)
     old = loadings_v[:, pl.ds(pl.multiple_of(z * GENES_Z, GENES_Z), GENES_Z)]
     own = old
     for k in range(1, T):
         own = jnp.where(t == k, pltpu.roll(old, LANES - k * OWN_GENES, 1), own)
     right[...] = jnp.concatenate(counts_sum[:4], axis=0) - packed[TRIANGLE:ROWS1, :] - RIDGE * own
-    new = own + solve(matrix, right, column, inverse)
+    new = own + solve(matrix, right, column_a, column_b, inverse)
     mean = jnp.sum(packed[ROWS1 : ROWS1 + 8, :] + counts_sum[4], axis=0, keepdims=True) * (
         2.0 / (CELLS * CELL_DEVICES)
     )
@@ -626,7 +677,8 @@
         totals_copy(d).wait_send()
     for d in range(1, T):
         local2_copy(d).wait_send()
-        piece_copy(d).wait_send()
+        piece_copy(0, d).wait_send()
+        piece_copy(1, d).wait_send()
     factors_out.wait()
     own_final.wait()
     for k in range(len(places)):
@@ -687,7 +739,8 @@
             pltpu.VMEM((ROWS2, LANES), F32),
             pltpu.VMEM((WIDTH * WIDTH, LANES), F32),
             pltpu.VMEM((WIDTH, LANES), F32),
-            pltpu.VMEM((2, 2, WIDTH, LANES), F32),
+            pltpu.VMEM((2, WIDTH, LANES), F32),
+            pltpu.VMEM((2, WIDTH, LANES), F32),
             pltpu.VMEM((WIDTH + 8, LANES), F32),
             pltpu.VMEM((Z, 4, 16, LANES), F32),
             pltpu.VMEM((T, LOCAL, LANES), F32),
@@ -698,12 +751,16 @@
             pltpu.VMEM((Z * CELLS, LANES), BF16),
             pltpu.VMEM((Z * CELLS, LANES), BF16),
             pltpu.VMEM((ROWS2, LANES), F32),
-            pltpu.VMEM((T, PIECE2, LANES), F32),
-            pltpu.VMEM((T, PIECE2, LANES), F32),
+            pltpu.VMEM((Z, 8, LANES), F32),
+            pltpu.VMEM((T, 48, LANES), F32),
+            pltpu.VMEM((T, 48, LANES), F32),
+            pltpu.VMEM((T, 40, LANES), F32),
+            pltpu.VMEM((T, 40, LANES), F32),
             pltpu.VMEM((8, LANES), F32),
-            dma((4,)), dma((2,)), dma((Z,)), dma((Z,)), dma((4,)), dma((4,)), dma((4,)), dma((4,)),
+            pltpu.SemaphoreType.REGULAR((9,)),
+            dma((4,)), dma((2,)), dma((Z,)), dma((Z,)), dma((8,)), dma((8,)), dma((4,)), dma((4,)),
             dma((1,)), dma((1,)), dma((4 + 2 * Z,)), dma((4 * Z,)), dma((2 * Z,)),
-            dma((T,)), dma((T,)), dma((Z,)), dma((Z,)), dma((T,)), dma((T,)),
+            dma((T,)), dma((T,)), dma((Z,)), dma((Z,)), dma((2 * T,)), dma((2 * T,)),
             dma((CELL_DEVICES,)), dma((CELL_DEVICES,)),
         ],
         compiler_params=pltpu.CompilerParams(

time: 47.9 us -> 46.7 us (0.975)
  Pallas kernels: 46.7 us -> 46 us
    pallas_call x1, Pallas kernels: 44.8 us -> 44 us  [on_device(): pl.pallas_call(kernel, out_shape=(jax.ShapeDtypeStruct((WIDTH, CELLS), F3...]
where the time goes in v4:
time: 46.7 us; the launch traced here: 46.6 us
  Pallas kernels  46 us (99%)
  between operations  0.64 us (1%)
    pallas_call x1, Pallas kernels, on_device(): pl.pallas_call(kernel, out_shape=(jax.ShapeDtypeStruct((WIDTH, CELLS), F3...  44 us
    pallas_call x1, Pallas kernels, on_device(): pl.pallas_call(unpack, out_shape=(jax.ShapeDtypeStruct((WIDTH, CELLS), F3...  1.99 us

profile of v4, /device:TPU:8, one launch (start us, length us, event | category | flops | bytes accessed | tf_op | source)
XLA Modules:
  0.0 46.6 jit_solution(18206854678310928102)
XLA Ops:
  0.6 44.0 %sweep.1 = (f32[32,256]{1,0:T(8,128)}, f32[8,8,8,128]{3,2,1,0:T(8,128)}) custom-call(s32[256,1024]{1,0:T(8,128)} %counts_hbm.1, s32[2,128]{1,0:T(2,128)} %bitcast.8, f32[32,256]{1,0:T(8,128)} %bitcast.7, f32[32,1024]{1,0:T(8,128)} %bitcast.6), custom_call_target="tpu_custom_call" | custom-call | tf_op jit(solution)/shard_map/sweep/pallas_call | solution.py:713
  44.6 2.0 %unpack.1 = (f32[32,256]{1,0:T(8,128)}, f32[32,1024]{1,0:T(8,128)}, f32[8,128]{1,0:T(8,128)}) custom-call(f32[8,8,8,128]{3,2,1,0:T(8,128)} %get-tuple-element.8.final_ref, f32[32,256]{1,0:T(8,128)} %get-tuple-element.9.factors_ref), custom_call_target="tpu_custom_call" | custom-call | tf_op jit(solution)/shard_map/unpack/pallas_call | solution.py:771

commit v5 on v4

--- a/solution.py
+++ b/solution.py
@@ -25,8 +25,9 @@
 OWN_GENES = GENES_Z // T
 HALF = LANES // 2
 CHUNK = 128
-ORDER = (0, 1, 7, 2, 6, 3, 5, 4)
-FAR_FIRST = ORDER[:0:-1]
+ORDER = (0, 1, 7, 3, 5, 4, 2, 6)
+FAR_FIRST = (4, 3, 5, 2, 6, 1, 7)
+SENT = (1, 7, 4, 3, 5, 2, 6)
 PLANE = ((0, 0), (2, 1), (1, 1), (3, 1), (2, 0), (0, 1), (1, 0), (3, 0))
 
 HEIGHT = [WIDTH - c // 8 * 8 for c in range(WIDTH)]
@@ -86,51 +87,38 @@
     matrix_ref[pl.ds(0, WIDTH, stride=WIDTH + 1), :] = diagonal + shift
     row = lax.broadcasted_iota(jnp.int32, (WIDTH, LANES), 0)
 
-    def enter(c, at, column_ref, first, second):
+    def enter(c, column_ref, first, second):
         column_ref[0] = first
-        pivot = 1.0 / column_ref[0, pl.ds(at, 1), :]
-        inverse_ref[pl.ds(c, 1), :] = pivot
-        first_scaled = jnp.where(row == at, 0.0, first * pivot)
-        second = second - first_scaled * column_ref[0, pl.ds(at + 1, 1), :]
+        pivot = 1.0 / column_ref[0, c : c + 1, :]
+        inverse_ref[c : c + 1, :] = pivot
+        first_scaled = jnp.where(row == c, 0.0, first * pivot)
+        second = second - first_scaled * column_ref[0, c + 1 : c + 2, :]
         column_ref[1] = second
-        pivot = 1.0 / column_ref[1, pl.ds(at + 1, 1), :]
-        inverse_ref[pl.ds(c + 1, 1), :] = pivot
-        return first_scaled, jnp.where(row == at + 1, 0.0, second * pivot)
-
-    def advance(c, scaled, column_ref, column_next_ref, group):
-        first, second = scaled
-        after = jnp.minimum(c + 2, WIDTH - 2)
-
-        def reduced(value, j):
+        pivot = 1.0 / column_ref[1, c + 1 : c + 2, :]
+        inverse_ref[c + 1 : c + 2, :] = pivot
+        return first_scaled, jnp.where(row == c + 1, 0.0, second * pivot)
+
+    first, second = enter(0, first_ref, matrix_ref[:WIDTH, :], matrix_ref[WIDTH : 2 * WIDTH, :])
+    for c in range(0, WIDTH, 2):
+        column_ref, other_ref = (first_ref, second_ref) if c % 4 == 0 else (second_ref, first_ref)
+
+        def reduced(j):
             return (
-                value
-                - first * column_ref[0, pl.ds(j, 1), :]
-                - second * column_ref[1, pl.ds(j, 1), :]
+                matrix_ref[WIDTH * j : WIDTH * j + WIDTH, :]
+                - first * column_ref[0, j : j + 1, :]
+                - second * column_ref[1, j : j + 1, :]
             )
 
-        start = pl.multiple_of(after * WIDTH, WIDTH)
-        scaled_after = enter(
-            c + 2, after, column_next_ref,
-            reduced(matrix_ref[pl.ds(start, WIDTH), :], after),
-            reduced(matrix_ref[pl.ds(start + WIDTH, WIDTH), :], after + 1),
-        )
+        if c + 2 < WIDTH:
+            after = enter(c + 2, other_ref, reduced(c + 2), reduced(c + 3))
         value = right_ref[...]
-        value = value - first * right_ref[pl.ds(c, 1), :]
+        value = value - first * right_ref[c : c + 1, :]
         right_ref[...] = value
-        right_ref[...] = value - second * right_ref[pl.ds(c + 1, 1), :]
-        for j in range(8 * group, WIDTH):
-            at = slice(WIDTH * j, WIDTH * j + WIDTH)
-            matrix_ref[at, :] = reduced(matrix_ref[at, :], j)
-        return scaled_after
-
-    scaled = enter(0, 0, first_ref, matrix_ref[:WIDTH, :], matrix_ref[WIDTH : 2 * WIDTH, :])
-    for group in range(WIDTH // 8):
-
-        def step(quad, scaled):
-            scaled = advance(4 * quad, scaled, first_ref, second_ref, group)
-            return advance(4 * quad + 2, scaled, second_ref, first_ref, group)
-
-        scaled = lax.fori_loop(2 * group, 2 * group + 2, step, scaled)
+        right_ref[...] = value - second * right_ref[c + 1 : c + 2, :]
+        for j in range(c + 4, WIDTH):
+            matrix_ref[WIDTH * j : WIDTH * j + WIDTH, :] = reduced(j)
+        if c + 2 < WIDTH:
+            first, second = after
     return right_ref[...] * inverse_ref[:WIDTH, :]
 
 
@@ -407,10 +395,10 @@
     for step in range(1, 4):
         near_copy(step).start()
     told(4, 6)
-    for d in FAR_FIRST:
+    for d in SENT:
         for side in range(2):
             far_copy(d, side).start()
-    for d in FAR_FIRST:
+    for d in SENT:
         totals_copy(d).start()
 
     def factors_of(d):

time: 46.7 us -> 45.8 us (0.981)
  Pallas kernels: 46 us -> 45 us
    pallas_call x1, Pallas kernels: 44 us -> 43 us  [on_device(): pl.pallas_call(kernel, out_shape=(jax.ShapeDtypeStruct((WIDTH, CELLS), F3...]
where the time goes in v5:
time: 45.8 us; the launch traced here: 45.7 us
  Pallas kernels  45 us (98%)
  between operations  0.64 us (1%)
    pallas_call x1, Pallas kernels, on_device(): pl.pallas_call(kernel, out_shape=(jax.ShapeDtypeStruct((WIDTH, CELLS), F3...  43 us
    pallas_call x1, Pallas kernels, on_device(): pl.pallas_call(unpack, out_shape=(jax.ShapeDtypeStruct((WIDTH, CELLS), F3...  1.99 us

profile of v5, /device:TPU:8, one launch (start us, length us, event | category | flops | bytes accessed | tf_op | source)
XLA Modules:
  0.0 45.7 jit_solution(15082993303169677795)
XLA Ops:
  0.6 43.0 %sweep.1 = (f32[32,256]{1,0:T(8,128)}, f32[8,8,8,128]{3,2,1,0:T(8,128)}) custom-call(s32[256,1024]{1,0:T(8,128)} %counts_hbm.1, s32[2,128]{1,0:T(2,128)} %bitcast.8, f32[32,256]{1,0:T(8,128)} %bitcast.7, f32[32,1024]{1,0:T(8,128)} %bitcast.6), custom_call_target="tpu_custom_call" | custom-call | tf_op jit(solution)/shard_map/sweep/pallas_call | solution.py:701
  43.7 2.0 %unpack.1 = (f32[32,256]{1,0:T(8,128)}, f32[32,1024]{1,0:T(8,128)}, f32[8,128]{1,0:T(8,128)}) custom-call(f32[8,8,8,128]{3,2,1,0:T(8,128)} %get-tuple-element.8.final_ref, f32[32,256]{1,0:T(8,128)} %get-tuple-element.9.factors_ref), custom_call_target="tpu_custom_call" | custom-call | tf_op jit(solution)/shard_map/unpack/pallas_call | solution.py:759

commit v6 on v5

--- a/solution.py
+++ b/solution.py
@@ -169,7 +169,7 @@
     right1, table1, high1, low1, counts_low, sums1, local1_out, local1_in, core_out, core_in,
     packed, matrix, right, column_a, column_b, inverse,
     factor_slots, local2_out, local2_in, local3_out, local3_in, table2, high2, low2, sums2, bases,
-    piece_out_a, piece_in_a, piece_out_b, piece_in_b,
+    piece_out, piece_in,
     final_out,
     rounds, input_sem, output_sem, totals_send, totals_recv, mirror_send, mirror_recv, local1_send, local1_recv, core_send, core_recv,
     factor_send, factor_recv, forward_send, local2_send, local2_recv, local3_send, local3_recv, piece_send, piece_recv,
@@ -539,7 +539,7 @@
     sums2[ROWS1 : ROWS1 + 8, :] = expected_sum
     sums2[ROWS1 + 8 :, :] = jnp.zeros((ROWS2 - ROWS1 - 8, LANES), F32)
 
-    parts = ((0, 48, piece_out_a, piece_in_a), (T * 48, 40, piece_out_b, piece_in_b))
+    parts = ((0, ROWS2 // T, piece_out, piece_in),)
 
     def piece_copy(part, d):
         target = plane(d)
@@ -666,7 +666,6 @@
     for d in range(1, T):
         local2_copy(d).wait_send()
         piece_copy(0, d).wait_send()
-        piece_copy(1, d).wait_send()
     factors_out.wait()
     own_final.wait()
     for k in range(len(places)):
@@ -740,10 +739,8 @@
             pltpu.VMEM((Z * CELLS, LANES), BF16),
             pltpu.VMEM((ROWS2, LANES), F32),
             pltpu.VMEM((Z, 8, LANES), F32),
-            pltpu.VMEM((T, 48, LANES), F32),
-            pltpu.VMEM((T, 48, LANES), F32),
-            pltpu.VMEM((T, 40, LANES), F32),
-            pltpu.VMEM((T, 40, LANES), F32),
+            pltpu.VMEM((T, ROWS2 // T, LANES), F32),
+            pltpu.VMEM((T, ROWS2 // T, LANES), F32),
             pltpu.VMEM((8, LANES), F32),
             pltpu.SemaphoreType.REGULAR((9,)),
             dma((4,)), dma((2,)), dma((Z,)), dma((Z,)), dma((8,)), dma((8,)), dma((4,)), dma((4,)),

time: 45.8 us -> 46.5 us (1.015)
  the two profiles are of different devices: /device:TPU:8 before, /device:TPU:1 now
where the time goes in v6:
time: 46.5 us; the launch traced here: 46.4 us
  Pallas kernels  45.8 us (98%)
  between operations  0.64 us (1%)
    pallas_call x1, Pallas kernels, on_device(): pl.pallas_call(kernel, out_shape=(jax.ShapeDtypeStruct((WIDTH, CELLS), F3...  43.8 us
    pallas_call x1, Pallas kernels, on_device(): pl.pallas_call(unpack, out_shape=(jax.ShapeDtypeStruct((WIDTH, CELLS), F3...  1.99 us

profile of v6, /device:TPU:1, one launch (start us, length us, event | category | flops | bytes accessed | tf_op | source)
XLA Modules:
  0.0 46.4 jit_solution(10290695411737549759)
XLA Ops:
  0.6 43.8 %sweep.1 = (f32[32,256]{1,0:T(8,128)}, f32[8,8,8,128]{3,2,1,0:T(8,128)}) custom-call(s32[256,1024]{1,0:T(8,128)} %counts_hbm.1, s32[2,128]{1,0:T(2,128)} %bitcast.8, f32[32,256]{1,0:T(8,128)} %bitcast.7, f32[32,1024]{1,0:T(8,128)} %bitcast.6), custom_call_target="tpu_custom_call" | custom-call | tf_op jit(solution)/shard_map/sweep/pallas_call | solution.py:700
  44.4 2.0 %unpack.1 = (f32[32,256]{1,0:T(8,128)}, f32[32,1024]{1,0:T(8,128)}, f32[8,128]{1,0:T(8,128)}) custom-call(f32[8,8,8,128]{3,2,1,0:T(8,128)} %get-tuple-element.8.final_ref, f32[32,256]{1,0:T(8,128)} %get-tuple-element.9.factors_ref), custom_call_target="tpu_custom_call" | custom-call | tf_op jit(solution)/shard_map/unpack/pallas_call | solution.py:756
